TPU v7x, 32 devices: a whole 2x2x4 slice. The times are simulated.
32 devices in a mesh: lat: 8 (over y, x, core), lon: 4 (over z).
Axes of the slice: x: 2, y: 2, z: 4, core: 2. Of those that a mesh axis runs over, the one named last changes fastest.
Arguments:
- right_side: float32 [128, 2560], P('lat', 'lon'), may hold values from -34 to 34
- first_guess: float32 [128, 2560], P('lat', 'lon'), may hold values from -3 to 3
- cell_mask: int32 [128, 2560], P('lat', 'lon'), may hold values 0 or 1
- cond_east: float32 [128, 2560], P('lat', 'lon'), may hold values from 0.5 to 2
- cond_north: float32 [128, 2560], P('lat', 'lon'), may hold values from 0.5 to 2
- surface: float32 [128, 2560], P('lat', 'lon'), may hold values from 0.02 to 0.5
- recycled: float32 [16, 128, 2560], P(None, 'lat', 'lon'), may hold values from -0.0031444706 to 0.0031444706
Outputs:
- solution: float32 [128, 2560], P('lat', 'lon')
- residual: float32 [128, 2560], P('lat', 'lon')
All inputs are finite; a program needn't handle non-finite values. No bound on the sum of `cell_mask` on one device may be relied on, other than what follows from the above.
Results may differ from a plain program's by a relative error of at most 0.0003.
Values sent between devices are 32-bit elements; how exact they have to be, the bound alone decides.
No kernel may reach another device: no remote copies, remote signals or barrier semaphores. Data moves between devices by JAX's collectives and lax.ppermute only.
A program may use at most 64 MiB of HBM per device.

v0:
```python
import jax
import jax.numpy as jnp
from jax import lax
from jax.sharding import PartitionSpec as P

ITERS = 3


PRECISE = lax.Precision.HIGHEST


def with_halo(block, sides, width):
    for axis, dim in sides:
        count = lax.axis_size(axis)
        forward = [(i, i + 1) for i in range(count - 1)]
        forward.append((count - 1, 0))
        backward = [(target, source) for source, target in forward]
        low = lax.ppermute(
            lax.slice_in_dim(block, block.shape[dim] - width, None, axis=dim), axis, forward
        )
        high = lax.ppermute(lax.slice_in_dim(block, 0, width, axis=dim), axis, backward)
        block = jnp.concatenate([low, block, high], axis=dim)
    return block


def close_poles(padded):
    row_index = lax.axis_index("lat")
    last_row = lax.axis_size("lat") - 1
    keep_south = (row_index > 0).astype(jnp.float32)
    keep_north = (row_index < last_row).astype(jnp.float32)
    return jnp.concatenate(
        [padded[..., :1, :] * keep_south, padded[..., 1:-1, :], padded[..., -1:, :] * keep_north],
        axis=-2,
    )


def faces(side, surface):
    wet_pad = side[0]
    east_pad = side[1]
    north_pad = side[2]
    wet_cells = wet_pad[1:-1, 1:-1]
    k_east = east_pad[1:-1, 1:-1] * wet_pad[1:-1, 2:]
    k_west = east_pad[1:-1, :-2] * wet_cells
    k_north = north_pad[1:-1, 1:-1] * wet_pad[2:, 1:-1]
    k_south = north_pad[:-2, 1:-1] * wet_cells
    centre = surface * wet_cells + k_east + k_west + k_north + k_south + (1.0 - wet_cells)
    return (centre, k_east, k_west, k_north, k_south)


def operate_padded(padded, coeffs):
    centre, k_east, k_west, k_north, k_south = coeffs
    inner = padded[..., 1:-1, 1:-1]
    to_east = padded[..., 1:-1, 2:]
    to_west = padded[..., 1:-1, :-2]
    to_north = padded[..., 2:, 1:-1]
    to_south = padded[..., :-2, 1:-1]
    return centre * inner - (
        k_east * to_east + k_west * to_west + k_north * to_north + k_south * to_south
    )


def residual_image(residual, coeffs):
    padded = with_halo(residual, (("lat", 0), ("lon", 1)), 1)
    return operate_padded(padded, coeffs)


def solve_small(factor, target):
    return jax.scipy.linalg.cho_solve((factor, True), target)


def shards(right_side, first_guess, cell_mask, cond_east, cond_north, surface, recycled):
    wet_cells = cell_mask.astype(jnp.float32)
    local_side = jnp.stack([wet_cells, cond_east * wet_cells, cond_north * wet_cells, first_guess])
    padded_all = with_halo(
        jnp.concatenate([local_side, recycled], axis=0), (("lat", 1), ("lon", 2)), 1
    )
    side_pad = close_poles(padded_all[:3])
    guess_pad = padded_all[3]
    basis_pad = padded_all[4:]
    coeffs = faces(side_pad, surface)
    basis_image = operate_padded(basis_pad, coeffs)
    start_res = right_side - operate_padded(guess_pad, coeffs)
    gram_local = jnp.einsum("kyx,lyx->kl", recycled, basis_image, precision=PRECISE)
    start_local = jnp.einsum("kyx,yx->k", recycled, start_res, precision=PRECISE)
    gram, start = lax.psum((gram_local, start_local), ("lat", "lon"))
    factor = jnp.linalg.cholesky(0.5 * (gram + gram.T))
    coarse = solve_small(factor, start)
    solution = first_guess + jnp.einsum("kyx,k->yx", recycled, coarse, precision=PRECISE)
    residual = start_res - jnp.einsum("kyx,k->yx", basis_image, coarse, precision=PRECISE)
    direction = residual
    dir_image = residual
    curv = jnp.float32(1.0)
    prev_norm = jnp.float32(1.0)
    for turn_index in range(ITERS):
        image_res = residual_image(residual, coeffs)
        defl_local = jnp.einsum("kyx,yx->k", recycled, image_res, precision=PRECISE)
        res_norm, res_image, defl = lax.psum(
            (jnp.sum(residual * residual), jnp.sum(residual * image_res), defl_local),
            ("lat", "lon"),
        )
        coef = solve_small(factor, defl)
        along_basis = jnp.einsum("kyx,k->yx", recycled, coef, precision=PRECISE)
        along_image = jnp.einsum("kyx,k->yx", basis_image, coef, precision=PRECISE)
        if turn_index == 0:
            direction = residual - along_basis
            dir_image = image_res - along_image
            curv = res_image - jnp.sum(coef * defl)
        else:
            ratio = res_norm / prev_norm
            direction = residual - along_basis + ratio * direction
            dir_image = image_res - along_image + ratio * dir_image
            curv = res_image - jnp.sum(coef * defl) - ratio * ratio * curv
        step_len = res_norm / curv
        solution = solution + step_len * direction
        residual = residual - step_len * dir_image
        prev_norm = res_norm
    return (solution, residual)


def solution(mesh):
    return jax.shard_map(
        shards,
        mesh=mesh,
        in_specs=(
            P("lat", "lon"),
            P("lat", "lon"),
            P("lat", "lon"),
            P("lat", "lon"),
            P("lat", "lon"),
            P("lat", "lon"),
            P(None, "lat", "lon"),
        ),
        out_specs=(P("lat", "lon"), P("lat", "lon")),
        check_vma=False,
    )
```

profile of v0, /device:TPU:0, one launch (start us, length us, event | category | flops | bytes accessed | tf_op | source)
XLA Modules:
  0.0 244.8 jit_solution(5248051123626684629)
XLA Ops:
  0.6 0.8 bitcast_dynamic-update-slice_fusion.3
  3.1 1.1 constant_dynamic-update-slice_fusion
  4.3 3.4 %collective-permute-start.1 = (f32[20,1,640]{2,1,0:T(1,128)S(1)}, f32[20,1,640]{2,1,0:T(1,128)S(1)}, u32[]{:S(2)}, u32[]{:S(2)}) collective-permute-start(f32[20,1,640]{2,1,0:T(1,128)S(1)} %get-tuple-element.36), channel_id=1, source_target_pairs={{4,0},{8,4},{12,8},{16,12},{20,16},{24,20},{28,24},{0,28},{5,1},{9... | collective-permute-start | bytes 153608 | tf_op jit(solution)/shard_map/ppermute | solution.py:21
  7.7 1.8 collective-permute-done.1
  9.5 2.7 %collective-permute-done = f32[20,1,640]{2,1,0:T(1,128)S(1)} collective-permute-done((f32[20,1,640]{2,1,0:T(1,128)S(1)}, f32[20,1,640]{2,1,0:T(1,128)S(1)}, u32[]{:S(2)}, u32[]{:S(2)}) %collective-permute-start) | collective-permute-done | bytes 51232 | tf_op jit(solution)/shard_map/ppermute | solution.py:18
  12.3 3.7 %collective-permute-start.3 = (f32[20,18,1]{2,1,0:T(8,128)S(1)}, f32[20,18,1]{2,1,0:T(8,128)S(1)}, u32[]{:S(2)}, u32[]{:S(2)}) collective-permute-start(f32[20,18,1]{2,1,0:T(8,128)S(1)} %get-tuple-element.34), channel_id=1, source_target_pairs={{1,0},{2,1},{3,2},{0,3},{5,4},{6,5},{7,6},{4,7},{9,8},{10,9},{11,1... | collective-permute-start | bytes 4328 | tf_op jit(solution)/shard_map/ppermute | solution.py:21
  16.0 5.2 %collective-permute-done.3 = f32[20,18,1]{2,1,0:T(8,128)S(1)} collective-permute-done((f32[20,18,1]{2,1,0:T(8,128)S(1)}, f32[20,18,1]{2,1,0:T(8,128)S(1)}, u32[]{:S(2)}, u32[]{:S(2)}) %collective-permute-start.3) | collective-permute-done | bytes 1472 | tf_op jit(solution)/shard_map/ppermute | solution.py:21
  21.1 3.9 %collective-permute-done.2 = f32[20,18,1]{2,1,0:T(8,128)S(1)} collective-permute-done((f32[20,18,1]{2,1,0:T(8,128)S(1)}, f32[20,18,1]{2,1,0:T(8,128)S(1)}, u32[]{:S(2)}, u32[]{:S(2)}) %collective-permute-start.2) | collective-permute-done | bytes 1472 | tf_op jit(solution)/shard_map/ppermute | solution.py:18
  27.3 1.2 convolution_bitcast_fusion
  28.5 1.0 convolution_bitcast_fusion.9
  29.4 40.8 %all-reduce.3 = (f32[16,16]{0,1:T(8,128)S(1)}, f32[16]{0:T(128)S(1)}) all-reduce(f32[16,16]{0,1:T(8,128)S(1)} %convolution_bitcast_fusion, f32[16]{0:T(128)S(1)} %convolution_bitcast_fusion.9), channel_id=1, replica_groups=mesh['lat'=8,'lon'=4] {'lat','lon'}, use_global_device_ids=true, to_apply=%region_0.0 | all-reduce | flops 272 | bytes 2176 | tf_op jit(solution)/shard_map/psum | solution.py:85
  70.4 1.5 cholesky.18
  73.2 1.2 custom-call.11
  75.4 2.6 %collective-permute-start.5 = (f32[1,640]{1,0:T(1,128)S(1)}, f32[1,640]{1,0:T(1,128)S(1)}, u32[]{:S(2)}, u32[]{:S(2)}) collective-permute-start(f32[1,640]{1,0:T(1,128)S(1)} %get-tuple-element.52), channel_id=1, source_target_pairs={{4,0},{8,4},{12,8},{16,12},{20,16},{24,20},{28,24},{0,28},{5,1},{9... | collective-permute-start | bytes 7688 | tf_op jit(solution)/shard_map/ppermute | solution.py:21
  79.9 3.4 %collective-permute-start.6 = (f32[18,1]{1,0:T(8,128)S(1)}, f32[18,1]{1,0:T(8,128)S(1)}, u32[]{:S(2)}, u32[]{:S(2)}) collective-permute-start(f32[18,1]{1,0:T(8,128)S(1)} %get-tuple-element.44), channel_id=1, source_target_pairs={{1,0},{2,1},{3,2},{0,3},{5,4},{6,5},{7,6},{4,7},{9,8},{10,9},{11,1... | collective-permute-start | bytes 224 | tf_op jit(solution)/shard_map/ppermute | solution.py:21
  83.3 1.7 collective-permute-done.7
  85.7 0.9 convolution_bitcast_fusion.6
  86.6 39.8 %all-reduce.2 = (f32[]{:T(128)}, f32[]{:T(128)}, f32[16]{0:T(128)S(1)}) all-reduce(f32[]{:T(128)} %get-tuple-element.8, f32[]{:T(128)} %get-tuple-element.7, f32[16]{0:T(128)S(1)} %convolution_bitcast_fusion.6), channel_id=1, replica_groups=mesh['lat'=8,'lon'=4] {'lat','lon'}, use_global_device_ids=true, to_apply=%region_5.7 | all-reduce | flops 18 | bytes 144 | tf_op jit(solution)/shard_map/psum | solution.py:97
  130.0 2.6 %collective-permute-start.9 = (f32[1,640]{1,0:T(1,128)S(1)}, f32[1,640]{1,0:T(1,128)S(1)}, u32[]{:S(2)}, u32[]{:S(2)}) collective-permute-start(f32[1,640]{1,0:T(1,128)S(1)} %get-tuple-element.50), channel_id=1, source_target_pairs={{4,0},{8,4},{12,8},{16,12},{20,16},{24,20},{28,24},{0,28},{5,1},{9... | collective-permute-start | bytes 7688 | tf_op jit(solution)/shard_map/ppermute | solution.py:21
  134.0 2.1 collective-permute-start.11
  136.1 1.7 collective-permute-start.10
  137.8 1.7 collective-permute-done.11
  140.6 0.9 convolution_bitcast_fusion.4
  141.5 40.9 %all-reduce.1 = (f32[16]{0:T(128)S(1)}, f32[]{:T(128)}, f32[]{:T(128)}) all-reduce(f32[16]{0:T(128)S(1)} %convolution_bitcast_fusion.4, f32[]{:T(128)} %get-tuple-element.6, f32[]{:T(128)} %get-tuple-element.5), channel_id=1, replica_groups=mesh['lat'=8,'lon'=4] {'lat','lon'}, use_global_device_ids=true, to_apply=%region_14.16 | all-reduce | flops 18 | bytes 144 | tf_op jit(solution)/shard_map/psum | solution.py:97
  182.6 0.8 fusion.99
  187.4 2.6 %collective-permute-start.13 = (f32[1,640]{1,0:T(1,128)S(1)}, f32[1,640]{1,0:T(1,128)S(1)}, u32[]{:S(2)}, u32[]{:S(2)}) collective-permute-start(f32[1,640]{1,0:T(1,128)S(1)} %get-tuple-element.48), channel_id=1, source_target_pairs={{4,0},{8,4},{12,8},{16,12},{20,16},{24,20},{28,24},{0,28},{5,1},{9... | collective-permute-start | bytes 7688 | tf_op jit(solution)/shard_map/ppermute | solution.py:21
  191.4 1.9 collective-permute-start.15
  193.3 1.9 collective-permute-start.14
  195.3 1.7 collective-permute-done.15
  197.8 0.9 convolution_bitcast_fusion.2
  198.7 39.9 %all-reduce = (f32[16]{0:T(128)S(1)}, f32[]{:T(128)}, f32[]{:T(128)}) all-reduce(f32[16]{0:T(128)S(1)} %convolution_bitcast_fusion.2, f32[]{:T(128)} %get-tuple-element.4, f32[]{:T(128)} %get-tuple-element.3), channel_id=1, replica_groups=mesh['lat'=8,'lon'=4] {'lat','lon'}, use_global_device_ids=true, to_apply=%region_20.22 | all-reduce | flops 18 | bytes 144 | tf_op jit(solution)/shard_map/psum | solution.py:97
  238.8 0.8 fusion.97
  (73 shorter events, 18.1 us)
Async XLA Ops:
  0.6 0.9 copy-start.1
  0.6 0.9 copy-start.5
  1.5 0.8 copy-start.6
  2.3 0.8 copy-start.2
  4.3 5.2 %collective-permute-start.1 = (f32[20,1,640]{2,1,0:T(1,128)S(1)}, f32[20,1,640]{2,1,0:T(1,128)S(1)}, u32[]{:S(2)}, u32[]{:S(2)}) collective-permute-start(f32[20,1,640]{2,1,0:T(1,128)S(1)} %get-tuple-element.36), channel_id=1, source_target_pairs={{4,0},{8,4},{12,8},{16,12},{20,16},{24,20},{28,24},{0,28},{5,1},{9... | collective-permute-start | bytes 153608 | tf_op jit(solution)/shard_map/ppermute | solution.py:21
  7.7 4.4 %collective-permute-start = (f32[20,1,640]{2,1,0:T(1,128)S(1)}, f32[20,1,640]{2,1,0:T(1,128)S(1)}, u32[]{:S(2)}, u32[]{:S(2)}) collective-permute-start(f32[20,1,640]{2,1,0:T(1,128)S(1)} %get-tuple-element.35), channel_id=1, source_target_pairs={{0,4},{4,8},{8,12},{12,16},{16,20},{20,24},{24,28},{28,0},{1,5},{5... | collective-permute-start | bytes 153608 | tf_op jit(solution)/shard_map/ppermute | solution.py:18
  12.3 8.8 %collective-permute-start.3 = (f32[20,18,1]{2,1,0:T(8,128)S(1)}, f32[20,18,1]{2,1,0:T(8,128)S(1)}, u32[]{:S(2)}, u32[]{:S(2)}) collective-permute-start(f32[20,18,1]{2,1,0:T(8,128)S(1)} %get-tuple-element.34), channel_id=1, source_target_pairs={{1,0},{2,1},{3,2},{0,3},{5,4},{6,5},{7,6},{4,7},{9,8},{10,9},{11,1... | collective-permute-start | bytes 4328 | tf_op jit(solution)/shard_map/ppermute | solution.py:21
  16.0 9.1 %collective-permute-start.2 = (f32[20,18,1]{2,1,0:T(8,128)S(1)}, f32[20,18,1]{2,1,0:T(8,128)S(1)}, u32[]{:S(2)}, u32[]{:S(2)}) collective-permute-start(f32[20,18,1]{2,1,0:T(8,128)S(1)} %get-tuple-element.33), channel_id=1, source_target_pairs={{0,1},{1,2},{2,3},{3,0},{4,5},{5,6},{6,7},{7,4},{8,9},{9,10},{10,1... | collective-permute-start | bytes 4328 | tf_op jit(solution)/shard_map/ppermute | solution.py:18
  25.4 0.8 copy-start.3
  25.4 0.8 copy-start.4
  25.5 1.1 copy-start
  75.4 4.0 %collective-permute-start.4 = (f32[1,640]{1,0:T(1,128)S(1)}, f32[1,640]{1,0:T(1,128)S(1)}, u32[]{:S(2)}, u32[]{:S(2)}) collective-permute-start(f32[1,640]{1,0:T(1,128)S(1)} %get-tuple-element.53), channel_id=1, source_target_pairs={{0,4},{4,8},{8,12},{12,16},{16,20},{20,24},{24,28},{28,0},{1,5},{5... | collective-permute-start | bytes 7688 | tf_op jit(solution)/shard_map/ppermute | solution.py:18
  75.4 3.9 %collective-permute-start.5 = (f32[1,640]{1,0:T(1,128)S(1)}, f32[1,640]{1,0:T(1,128)S(1)}, u32[]{:S(2)}, u32[]{:S(2)}) collective-permute-start(f32[1,640]{1,0:T(1,128)S(1)} %get-tuple-element.52), channel_id=1, source_target_pairs={{4,0},{8,4},{12,8},{16,12},{20,16},{24,20},{28,24},{0,28},{5,1},{9... | collective-permute-start | bytes 7688 | tf_op jit(solution)/shard_map/ppermute | solution.py:21
  79.5 5.5 %collective-permute-start.7 = (f32[18,1]{1,0:T(8,128)S(1)}, f32[18,1]{1,0:T(8,128)S(1)}, u32[]{:S(2)}, u32[]{:S(2)}) collective-permute-start(f32[18,1]{1,0:T(8,128)S(1)} %get-tuple-element.45), channel_id=1, source_target_pairs={{0,1},{1,2},{2,3},{3,0},{4,5},{5,6},{6,7},{7,4},{8,9},{9,10},{10,1... | collective-permute-start | bytes 224 | tf_op jit(solution)/shard_map/ppermute | solution.py:18
  79.9 5.1 %collective-permute-start.6 = (f32[18,1]{1,0:T(8,128)S(1)}, f32[18,1]{1,0:T(8,128)S(1)}, u32[]{:S(2)}, u32[]{:S(2)}) collective-permute-start(f32[18,1]{1,0:T(8,128)S(1)} %get-tuple-element.44), channel_id=1, source_target_pairs={{1,0},{2,1},{3,2},{0,3},{5,4},{6,5},{7,6},{4,7},{9,8},{10,9},{11,1... | collective-permute-start | bytes 224 | tf_op jit(solution)/shard_map/ppermute | solution.py:21
  129.9 4.0 %collective-permute-start.8 = (f32[1,640]{1,0:T(1,128)S(1)}, f32[1,640]{1,0:T(1,128)S(1)}, u32[]{:S(2)}, u32[]{:S(2)}) collective-permute-start(f32[1,640]{1,0:T(1,128)S(1)} %get-tuple-element.51), channel_id=1, source_target_pairs={{0,4},{4,8},{8,12},{12,16},{16,20},{20,24},{24,28},{28,0},{1,5},{5... | collective-permute-start | bytes 7688 | tf_op jit(solution)/shard_map/ppermute | solution.py:18
  130.0 3.9 %collective-permute-start.9 = (f32[1,640]{1,0:T(1,128)S(1)}, f32[1,640]{1,0:T(1,128)S(1)}, u32[]{:S(2)}, u32[]{:S(2)}) collective-permute-start(f32[1,640]{1,0:T(1,128)S(1)} %get-tuple-element.50), channel_id=1, source_target_pairs={{4,0},{8,4},{12,8},{16,12},{20,16},{24,20},{28,24},{0,28},{5,1},{9... | collective-permute-start | bytes 7688 | tf_op jit(solution)/shard_map/ppermute | solution.py:21
  134.0 5.5 %collective-permute-start.11 = (f32[18,1]{1,0:T(8,128)S(1)}, f32[18,1]{1,0:T(8,128)S(1)}, u32[]{:S(2)}, u32[]{:S(2)}) collective-permute-start(f32[18,1]{1,0:T(8,128)S(1)} %get-tuple-element.43), channel_id=1, source_target_pairs={{0,1},{1,2},{2,3},{3,0},{4,5},{5,6},{6,7},{7,4},{8,9},{9,10},{10,1... | collective-permute-start | bytes 224 | tf_op jit(solution)/shard_map/ppermute | solution.py:18
  136.1 3.7 %collective-permute-start.10 = (f32[18,1]{1,0:T(8,128)S(1)}, f32[18,1]{1,0:T(8,128)S(1)}, u32[]{:S(2)}, u32[]{:S(2)}) collective-permute-start(f32[18,1]{1,0:T(8,128)S(1)} %get-tuple-element.42), channel_id=1, source_target_pairs={{1,0},{2,1},{3,2},{0,3},{5,4},{6,5},{7,6},{4,7},{9,8},{10,9},{11,1... | collective-permute-start | bytes 224 | tf_op jit(solution)/shard_map/ppermute | solution.py:21
  187.3 4.0 %collective-permute-start.12 = (f32[1,640]{1,0:T(1,128)S(1)}, f32[1,640]{1,0:T(1,128)S(1)}, u32[]{:S(2)}, u32[]{:S(2)}) collective-permute-start(f32[1,640]{1,0:T(1,128)S(1)} %get-tuple-element.49), channel_id=1, source_target_pairs={{0,4},{4,8},{8,12},{12,16},{16,20},{20,24},{24,28},{28,0},{1,5},{5... | collective-permute-start | bytes 7688 | tf_op jit(solution)/shard_map/ppermute | solution.py:18
  187.4 3.9 %collective-permute-start.13 = (f32[1,640]{1,0:T(1,128)S(1)}, f32[1,640]{1,0:T(1,128)S(1)}, u32[]{:S(2)}, u32[]{:S(2)}) collective-permute-start(f32[1,640]{1,0:T(1,128)S(1)} %get-tuple-element.48), channel_id=1, source_target_pairs={{4,0},{8,4},{12,8},{16,12},{20,16},{24,20},{28,24},{0,28},{5,1},{9... | collective-permute-start | bytes 7688 | tf_op jit(solution)/shard_map/ppermute | solution.py:21
  191.4 5.5 %collective-permute-start.15 = (f32[18,1]{1,0:T(8,128)S(1)}, f32[18,1]{1,0:T(8,128)S(1)}, u32[]{:S(2)}, u32[]{:S(2)}) collective-permute-start(f32[18,1]{1,0:T(8,128)S(1)} %get-tuple-element.41), channel_id=1, source_target_pairs={{0,1},{1,2},{2,3},{3,0},{4,5},{5,6},{6,7},{7,4},{8,9},{9,10},{10,1... | collective-permute-start | bytes 224 | tf_op jit(solution)/shard_map/ppermute | solution.py:18
  193.3 3.7 %collective-permute-start.14 = (f32[18,1]{1,0:T(8,128)S(1)}, f32[18,1]{1,0:T(8,128)S(1)}, u32[]{:S(2)}, u32[]{:S(2)}) collective-permute-start(f32[18,1]{1,0:T(8,128)S(1)} %get-tuple-element.40), channel_id=1, source_target_pairs={{1,0},{2,1},{3,2},{0,3},{5,4},{6,5},{7,6},{4,7},{9,8},{10,9},{11,1... | collective-permute-start | bytes 224 | tf_op jit(solution)/shard_map/ppermute | solution.py:21
where the time goes:
time: 246 us; the launch traced here: 245 us
  blocking collectives  161 us (65%)
  starting transfers between devices  26.6 us (11%)
  waiting for transfers between devices  21.1 us (9%)
  matrix products  13 us (5%)
  other arithmetic  9.43 us (4%)
  between operations  9.36 us (4%)
  local copies, waits for them, and re-layouts  3.82 us (2%)
    psum x3, blocking collectives, shards(): lax.psum((jnp.sum(residual * residual), jnp.sum(residual * image_res), de...  121 us
    psum x1, blocking collectives, shards(): gram, start = lax.psum((gram_local, start_local), ('lat', 'lon'))  40.8 us
    ppermute x8, starting transfers between devices, with_halo(): lax.ppermute(lax.slice_in_dim(block, 0, width, axis=dim), axis, backward)  22 us
    ppermute x8, waiting for transfers between devices, with_halo(): lax.ppermute(lax.slice_in_dim(block, block.shape[dim] - width, None, axis...  13.5 us
    ppermute x8, waiting for transfers between devices, with_halo(): lax.ppermute(lax.slice_in_dim(block, 0, width, axis=dim), axis, backward)  7.51 us
  transfers between devices with their start and end apart: 16, of which 12 were waited for; matrix products, arithmetic and copies ran while one was open for 1% of the time, Pallas kernels for 0%

commit v1 on v0

v1 whole, which is shorter than its diff:
```python
import functools

import jax
import jax.numpy as jnp
from jax import lax
from jax.experimental import pallas as pl
from jax.experimental.pallas import tpu as pltpu
from jax.sharding import PartitionSpec as P

SHIFT = 5.0
ITERS = 3
DEPTH = ITERS + 1
LANES = 128


def ring(count, step):
    return [(i, (i + step) % count) for i in range(count)]


def pack_kernel(basis, guess, rhs, mask, east, north, surf, to_n, to_s, to_e, to_w):
    vectors, rows, cols = basis.shape
    fields = [basis.at[k] for k in range(vectors)] + [guess, rhs, mask, east, north, surf]
    strip_e = jnp.zeros((rows, LANES), jnp.float32)
    strip_w = jnp.zeros((rows, LANES), jnp.float32)
    lane = lax.broadcasted_iota(jnp.int32, (rows, LANES), 1)
    for f, ref in enumerate(fields):
        at = DEPTH * f
        to_n[pl.ds(at, DEPTH), :] = ref[rows - DEPTH :, :].astype(jnp.float32)
        to_s[pl.ds(at, DEPTH), :] = ref[:DEPTH, :].astype(jnp.float32)
        here = (lane >= at) & (lane < at + DEPTH)
        last = ref[:, cols - LANES :].astype(jnp.float32)
        first = ref[:, :LANES].astype(jnp.float32)
        strip_e = jnp.where(here, pltpu.roll(last, (at + DEPTH) % LANES, 1), strip_e)
        strip_w = jnp.where(here, pltpu.roll(first, at, 1), strip_w)
    to_e[...] = strip_e
    to_w[...] = strip_w


def roll_lanes(v, by):
    return pltpu.roll(v, by % v.shape[1], 1)


def roll_rows(v, by):
    return pltpu.roll(v, by % v.shape[0], 0)


def apply_faces(v, diag, k_east, k_north):
    flux_e = k_east * (v - roll_lanes(v, -1))
    flux_n = k_north * (v - roll_rows(v, -1))
    return diag * v + (flux_e - roll_lanes(flux_e, 1)) + (flux_n - roll_rows(flux_n, 1))


def moments_kernel(
    place, basis, guess, rhs, mask, east, north, surf,
    from_n, from_s, from_e, from_w, ne, nw, se, sw,
    copies, basis_ext, side_ext, powers, fields_ext,
):
    vectors, rows, cols = basis.shape
    wide = cols + LANES
    tall = rows + 2 * DEPTH
    lane = lax.broadcasted_iota(jnp.int32, (tall, LANES), 1)
    strip_e = jnp.concatenate([from_e[...], ne[:DEPTH, :], se[rows - DEPTH :, :]], axis=0)
    strip_w = jnp.concatenate([from_w[...], nw[:DEPTH, :], sw[rows - DEPTH :, :]], axis=0)

    def extend(f, own, out):
        at = DEPTH * f
        out[:rows, :cols] = own.astype(jnp.float32)
        out[rows : rows + DEPTH, :cols] = from_n[pl.ds(at, DEPTH), :]
        out[rows + DEPTH :, :cols] = from_s[pl.ds(at, DEPTH), :]
        edge_e = pltpu.roll(strip_e, (-at) % LANES, 1)
        edge_w = pltpu.roll(strip_w, (LANES - DEPTH - at) % LANES, 1)
        edge = jnp.where(lane < DEPTH, edge_e, jnp.where(lane >= LANES - DEPTH, edge_w, 0.0))
        out[:, cols:] = edge

    for k in range(vectors):
        extend(k, basis[k], basis_ext.at[k])
    for f, ref in enumerate((guess, rhs, mask, east, north, surf)):
        extend(vectors + f, ref[...], fields_ext.at[f])
    row = lax.broadcasted_iota(jnp.int32, (tall, wide), 0)
    beyond_n = (row >= rows) & (row < rows + DEPTH) & (place[0] == place[1] - 1)
    beyond_s = (row >= rows + DEPTH) & (place[0] == 0)
    wet = jnp.where(beyond_n | beyond_s, 0.0, fields_ext[2])
    k_east = fields_ext[3] * wet * roll_lanes(wet, -1)
    k_north = fields_ext[4] * wet * roll_rows(wet, -1)
    diag = fields_ext[5] * wet + (1.0 - wet)
    side_ext[0] = diag
    side_ext[1] = k_east
    side_ext[2] = k_north
    start = fields_ext[1] - apply_faces(fields_ext[0], diag, k_east, k_north)
    side_ext[3] = start

    def put(index, v):
        for tile in range(cols // LANES):
            at = tile * LANES
            powers[tile, pl.ds(index * rows, rows), :] = v[:rows, at : at + LANES]

    def shifted(v):
        return apply_faces(v, side_ext[0] - SHIFT, side_ext[1], side_ext[2])

    def one_vector(k, carry):
        v = basis_ext[k]
        put(k, v)
        v = apply_faces(v, side_ext[0], side_ext[1], side_ext[2])
        put(vectors + k, v)
        for power in range(ITERS):
            v = shifted(v)
            put((2 + power) * vectors + k, v)
        return carry

    lax.fori_loop(0, vectors, one_vector, 0)
    v = start
    base = (ITERS + 2) * vectors
    put(base, v)
    for power in range(ITERS):
        v = shifted(v)
        put(base + 1 + power, v)
    spare = 8 - (ITERS + 1)
    powers[:, pl.ds((base + ITERS + 1) * rows, spare * rows), :] = jnp.zeros(
        (cols // LANES, spare * rows, LANES), jnp.float32
    )
    count = base + 8
    nt = (((1,), (1,)), ((), ()))

    def one_row(r, carry):
        high_sum, cross_sum = carry
        tiles = range(cols // LANES)
        x = [powers[tile, pl.ds(r, count, stride=rows), :] for tile in tiles]
        x = jnp.concatenate(x, axis=1)
        high = x.astype(jnp.bfloat16)
        low = (x - high.astype(jnp.float32)).astype(jnp.bfloat16)
        high_sum += lax.dot_general(high, high, nt, preferred_element_type=jnp.float32)
        cross_sum += lax.dot_general(high, low, nt, preferred_element_type=jnp.float32)
        return high_sum, cross_sum

    zero = jnp.zeros((count, count), jnp.float32)
    high_sum, cross_sum = lax.fori_loop(0, rows, one_row, (zero, zero))
    full = high_sum + cross_sum + cross_sum.T
    full = jnp.concatenate([full, jnp.zeros((count, LANES - count), jnp.float32)], axis=1)
    at = lax.broadcasted_iota(jnp.int32, (vectors, LANES), 1)
    slabs = [full[a * vectors : (a + 1) * vectors, :] for a in range(4)]
    tail = jnp.concatenate([full[base:, :], jnp.zeros((vectors - 8, LANES), jnp.float32)], axis=0)
    out = jnp.zeros((vectors, LANES), jnp.float32)

    def move(out, v, first, width, target):
        moved = pltpu.roll(v, (target - first) % LANES, 1)
        return jnp.where((at >= target) & (at < target + width), moved, out)

    out = move(out, slabs[0], vectors, vectors, 0)
    out = move(out, slabs[1], vectors, 2 * vectors, vectors)
    out = move(out, slabs[2], 2 * vectors, 2 * vectors, 3 * vectors)
    out = move(out, slabs[3], 3 * vectors, 2 * vectors, 5 * vectors)
    free = 7 * vectors
    out = move(out, slabs[0], base, 1, free)
    out = move(out, slabs[1], base, 2, free + 1)
    out = move(out, slabs[2], base + 1, 2, free + 3)
    out = move(out, slabs[3], base + 2, 2, free + 5)
    out = move(out, tail, base, 4, free + 8)

    def one_copy(device, carry):
        copies[device] = out
        return carry

    lax.fori_loop(0, copies.shape[0], one_copy, 0, unroll=8)


def finish_kernel(parts, guess, basis_ext, side_ext, solution, residual, spread):
    vectors, tall, wide = basis_ext.shape
    rows, cols = guess.shape
    free = 7 * vectors
    several = 8

    def add_parts(i, sums):
        return tuple(sums[n] + parts[i * several + n] for n in range(several))

    nothing = (jnp.zeros(parts.shape[1:], jnp.float32),) * several
    sums = list(lax.fori_loop(0, parts.shape[0] // several, add_parts, nothing, unroll=2))
    while len(sums) > 1:
        sums = [sums[i] + sums[i + 1] for i in range(0, len(sums), 2)]
    total = sums[0]
    lane = lax.broadcasted_iota(jnp.int32, (vectors, LANES), 1)
    sub = lax.broadcasted_iota(jnp.int32, (vectors, LANES), 0)
    table = total
    for i in range(vectors):
        column = table[:, i : i + 1]
        pivot_row = table[i : i + 1, :] / table[i : i + 1, i : i + 1]
        table = jnp.where(sub == i, pivot_row, table - column * pivot_row)
    own_lane = (lane % vectors) == sub
    z = [-table[:, free : free + 1]]
    sums = jnp.zeros((vectors, LANES), jnp.float32)
    history = jnp.zeros((1, LANES), jnp.float32)
    lane_row = lane[:1, :]
    for j in range(2 * ITERS):
        newest = jnp.sum(jnp.where(own_lane, z[j], 0.0), axis=0, keepdims=True)
        history = pltpu.roll(history, vectors, 1)
        history = jnp.where((lane_row >= vectors) & (lane_row < 2 * vectors), newest, history)
        terms = (lane >= vectors) & (lane < (j + 2) * vectors)
        weights = jnp.where(terms, history, jnp.where(lane == free + 1 + j, 1.0, 0.0))
        z.append(-jnp.sum(table * weights, axis=1, keepdims=True))
    for j in range(2 * ITERS + 1):
        sums = sums + pltpu.roll(jnp.where(lane >= free, total, 0.0) * z[j], j, 1)
    picked = jnp.where((lane > free) & (lane < free + 7), sums, 0.0)
    for a in range(ITERS):
        moved = pltpu.roll(total, (a - 7) % LANES, 1)
        first = free + 1 + 2 * a
        picked += jnp.where((sub == a) & (lane >= first) & (lane < first + 2), moved, 0.0)
    moment_row = jnp.sum(picked, axis=0, keepdims=True)
    mu = [moment_row[:, free + 1 + k : free + 2 + k] for k in range(2 * ITERS)]
    for i in range(ITERS + 1):
        spread[i] = jnp.broadcast_to(z[i], (vectors, LANES))

    nil = jnp.zeros((1, 1), jnp.float32)
    rho = [nil + 1.0] + [nil] * ITERS
    gamma = [nil] * (ITERS + 1)
    delta = [nil] * ITERS
    curv = nil
    prev = nil
    for j in range(ITERS):
        norm = nil
        image = nil
        for a in range(j + 1):
            for b in range(j + 1):
                pair = rho[a] * rho[b]
                norm += pair * mu[a + b]
                image += pair * (mu[a + b + 1] + SHIFT * mu[a + b])
        if j == 0:
            gamma = list(rho)
            curv = image
        else:
            ratio = norm / prev
            gamma = [rho[i] + ratio * gamma[i] for i in range(ITERS + 1)]
            curv = image - ratio * ratio * curv
        step = norm / curv
        delta = [delta[i] + step * gamma[i] for i in range(ITERS)]
        below = [nil] + gamma[:ITERS]
        rho = [rho[i] - step * (SHIFT * gamma[i] + below[i]) for i in range(ITERS + 1)]
        prev = norm

    along = [[] for _ in range(ITERS + 1)]
    for tile in range(wide // LANES):
        acc = [jnp.zeros((tall, LANES), jnp.float32) for _ in range(ITERS + 1)]
        for k in range(vectors):
            w = basis_ext[k, :, pl.ds(tile * LANES, LANES)]
            for i in range(ITERS + 1):
                acc[i] = acc[i] + w * spread[i, pl.ds(k, 1), :]
        for i in range(ITERS + 1):
            along[i].append(acc[i])
    along = [jnp.concatenate(pieces, axis=1) for pieces in along]
    diag, k_east, k_north = side_ext[0], side_ext[1], side_ext[2]
    image = functools.partial(apply_faces, k_east=k_east, k_north=k_north)
    v = side_ext[3] + image(along[0], diag)
    x = guess[...] - along[0][:rows, :cols]
    r = rho[0] * v[:rows, :cols]
    for i in range(ITERS):
        x = x + delta[i] * (v + along[i + 1])[:rows, :cols]
        v = image(v, diag - SHIFT) + image(along[i + 1], diag)
        r = r + rho[i + 1] * v[:rows, :cols]
    solution[...] = x
    residual[...] = r


def call(kernel, out_shape, inputs, scratch=(), smem=0, name=None):
    specs = [pl.BlockSpec(memory_space=pltpu.SMEM)] * smem
    specs += [pl.BlockSpec(memory_space=pltpu.VMEM)] * (len(inputs) - smem)
    return pl.pallas_call(
        kernel,
        out_shape=out_shape,
        in_specs=specs,
        out_specs=[pl.BlockSpec(memory_space=pltpu.VMEM)] * len(out_shape),
        scratch_shapes=scratch,
        name=name,
        compiler_params=pltpu.CompilerParams(vmem_limit_bytes=24 * 1024 * 1024),
    )(*inputs)


def f32(*shape):
    return jax.ShapeDtypeStruct(shape, jnp.float32)


def shards(right_side, first_guess, cell_mask, cond_east, cond_north, surface, recycled):
    vectors, rows, cols = recycled.shape
    n_lat, n_lon = lax.axis_size("lat"), lax.axis_size("lon")
    devices = n_lat * n_lon
    fields = vectors + 6
    tall, wide = rows + 2 * DEPTH, cols + LANES
    own = (recycled, first_guess, right_side, cell_mask, cond_east, cond_north, surface)
    band, strip = f32(fields * DEPTH, cols), f32(rows, LANES)
    to_n, to_s, to_e, to_w = call(pack_kernel, [band, band, strip, strip], own, name="pack")
    north, south = ring(n_lat, 1), ring(n_lat, -1)
    from_w = lax.ppermute(to_e, "lon", ring(n_lon, 1))
    from_e = lax.ppermute(to_w, "lon", ring(n_lon, -1))
    from_s = lax.ppermute(to_n, "lat", north)
    from_n = lax.ppermute(to_s, "lat", south)
    se, sw = lax.ppermute(from_e, "lat", north), lax.ppermute(from_w, "lat", north)
    ne, nw = lax.ppermute(from_e, "lat", south), lax.ppermute(from_w, "lat", south)
    place = jnp.stack([lax.axis_index("lat"), jnp.int32(n_lat)])
    copies, basis_ext, side_ext = call(
        moments_kernel,
        [f32(devices, vectors, LANES), f32(vectors, tall, wide), f32(4, tall, wide)],
        (place,) + own + (from_n, from_s, from_e, from_w, ne, nw, se, sw),
        scratch=[
            pltpu.VMEM((cols // LANES, ((ITERS + 2) * vectors + 8) * rows, LANES), jnp.float32),
            pltpu.VMEM((6, tall, wide), jnp.float32),
        ],
        smem=1,
        name="moments",
    )
    parts = lax.all_to_all(copies, ("lat", "lon"), 0, 0)
    return call(
        finish_kernel,
        [f32(rows, cols), f32(rows, cols)],
        (parts, first_guess, basis_ext, side_ext),
        scratch=[pltpu.VMEM((ITERS + 1, vectors, LANES), jnp.float32)],
        name="finish",
    )


def solution(mesh):
    block = P("lat", "lon")
    return jax.shard_map(
        shards,
        mesh=mesh,
        in_specs=(block,) * 6 + (P(None, "lat", "lon"),),
        out_specs=(block, block),
        check_vma=False,
    )
```

time: 246 us -> 63.4 us (0.26)
  blocking collectives: 161 us -> 15.1 us
  Pallas kernels: 0 us -> 19.9 us
  waiting for transfers between devices: 21.1 us -> 4.1 us
  starting transfers between devices: 26.6 us -> 12.3 us
  matrix products: 13 us -> 0 us
  other arithmetic: 9.43 us -> 0.07 us
  between operations: 9.36 us -> 0.68 us
  local copies, waits for them, and re-layouts: 3.82 us -> 10.4 us
    psum x4 -> x0, blocking collectives: 161 us -> none  [the longest x3 121 us: shards(): lax.psum((jnp.sum(residual * residual), jnp.sum(residual * image_res), de...]
    pallas_call x0 -> x3, Pallas kernels: none -> 19.9 us  [call(): pl.pallas_call(kernel, out_shape=out_shape, in_specs=specs, out_specs=[pl...]
    ppermute x16 -> x8, waiting for transfers between devices: 21.1 us -> 4.1 us  [the longest x1 1.44 us: shards(): from_w = lax.ppermute(to_e, 'lon', ring(n_lon, 1))]
    all_to_all x0 -> x1, blocking collectives: none -> 15.1 us  [shards(): parts = lax.all_to_all(copies, ('lat', 'lon'), 0, 0)]
    ppermute x16 -> x8, starting transfers between devices: 26.6 us -> 12.3 us  [the longest x1 3.6 us: shards(): from_e = lax.ppermute(to_w, 'lon', ring(n_lon, -1))]
    dot_general x13 -> x0, matrix products: 9.97 us -> none  [the longest x3 2.84 us: shards(): defl_local = jnp.einsum('kyx,yx->k', recycled, image_res, precision=PRECISE)]
    unnamed x15 -> x28, local copies, waits for them, and re-layouts: 2.45 us -> 10.4 us
    another operation x5 -> x1, other arithmetic: 4.01 us -> 0.07 us  [shards(): place = jnp.stack([lax.axis_index('lat'), jnp.int32(n_lat)])]
  transfers between devices with their start and end apart: 16 -> 8, of which waited for: 12 -> 3; matrix products, arithmetic and copies ran while one was open for 1% -> 0% of each run, Pallas kernels for 0% -> 0%
where the time goes in v1:
time: 63.4 us; the launch traced here: 62.5 us
  Pallas kernels  19.9 us (31%)
  blocking collectives  15.1 us (24%)
  starting transfers between devices  12.3 us (19%)
  local copies, waits for them, and re-layouts  10.4 us (16%)
  waiting for transfers between devices  4.1 us (6%)
  between operations  0.68 us (1%)
    pallas_call x3, Pallas kernels, call(): pl.pallas_call(kernel, out_shape=out_shape, in_specs=specs, out_specs=[pl...  19.9 us
    all_to_all x1, blocking collectives, shards(): parts = lax.all_to_all(copies, ('lat', 'lon'), 0, 0)  15.1 us
    unnamed x28, local copies, waits for them, and re-layouts  10.4 us
    ppermute x1, starting transfers between devices, shards(): from_e = lax.ppermute(to_w, 'lon', ring(n_lon, -1))  3.6 us
    ppermute x1, starting transfers between devices, shards(): from_n = lax.ppermute(to_s, 'lat', south)  3.41 us
    ppermute x1, starting transfers between devices, shards(): lax.ppermute(from_w, 'lat', south)  2.64 us
    ppermute x1, starting transfers between devices, shards(): lax.ppermute(from_e, 'lat', south)  2.64 us
    ppermute x1, waiting for transfers between devices, shards(): from_w = lax.ppermute(to_e, 'lon', ring(n_lon, 1))  1.44 us
  transfers between devices with their start and end apart: 8, of which 3 were waited for; matrix products, arithmetic and copies ran while one was open for 0% of the time, Pallas kernels for 0%

profile of v1, /device:TPU:0, one launch (start us, length us, event | category | flops | bytes accessed | tf_op | source)
XLA Modules:
  0.0 62.5 jit_solution(7185131862073350644)
XLA Ops:
  0.6 1.1 %copy-done = f32[16,16,640]{2,1,0:T(8,128)S(1)} copy-done((f32[16,16,640]{2,1,0:T(8,128)S(1)}, f32[16,16,640]{2,1,0:T(8,128)}, u32[]{:S(2)}) %copy-start) | copy-done | bytes 655384
  1.7 0.8 %copy-done.2 = f32[16,640]{1,0:T(8,128)S(1)} copy-done((f32[16,640]{1,0:T(8,128)S(1)}, f32[16,640]{1,0:T(8,128)}, u32[]{:S(2)}) %copy-start.2) | copy-done | bytes 40984
  2.5 0.8 %copy-done.4 = f32[16,640]{1,0:T(8,128)S(1)} copy-done((f32[16,640]{1,0:T(8,128)S(1)}, f32[16,640]{1,0:T(8,128)}, u32[]{:S(2)}) %copy-start.4) | copy-done | bytes 40984
  3.3 0.8 %copy-done.6 = s32[16,640]{1,0:T(8,128)S(1)} copy-done((s32[16,640]{1,0:T(8,128)S(1)}, s32[16,640]{1,0:T(8,128)}, u32[]{:S(2)}) %copy-start.6) | copy-done | bytes 40984
  4.1 0.8 %copy-done.8 = f32[16,640]{1,0:T(8,128)S(1)} copy-done((f32[16,640]{1,0:T(8,128)S(1)}, f32[16,640]{1,0:T(8,128)}, u32[]{:S(2)}) %copy-start.8) | copy-done | bytes 40984
  4.8 0.8 %copy-done.10 = f32[16,640]{1,0:T(8,128)S(1)} copy-done((f32[16,640]{1,0:T(8,128)S(1)}, f32[16,640]{1,0:T(8,128)}, u32[]{:S(2)}) %copy-start.10) | copy-done | bytes 40984
  5.6 0.8 %copy-done.12 = f32[16,640]{1,0:T(8,128)S(1)} copy-done((f32[16,640]{1,0:T(8,128)S(1)}, f32[16,640]{1,0:T(8,128)}, u32[]{:S(2)}) %copy-start.12) | copy-done | bytes 40984
  6.4 0.2 pack.1
  6.6 3.4 %collective-permute-start = (f32[88,640]{1,0:T(8,128)S(1)}, f32[88,640]{1,0:T(8,128)S(1)}, u32[]{:S(2)}, u32[]{:S(2)}) collective-permute-start(f32[88,640]{1,0:T(8,128)S(1)} %get-tuple-element.9), channel_id=1, source_target_pairs={{0,28},{4,0},{8,4},{12,8},{16,12},{20,16},{24,20},{28,24},{1,29},{... | collective-permute-start | bytes 675848 | tf_op jit(solution)/shard_map/ppermute | solution.py:292
  10.0 0.0 collective-permute-start.1
  10.0 3.6 %collective-permute-start.2 = (f32[16,128]{1,0:T(8,128)S(1)}, f32[16,128]{1,0:T(8,128)S(1)}, u32[]{:S(2)}, u32[]{:S(2)}) collective-permute-start(f32[16,128]{1,0:T(8,128)S(1)} %get-tuple-element.11), channel_id=1, source_target_pairs={{0,3},{1,0},{2,1},{3,2},{4,7},{5,4},{6,5},{7,6},{8,11},{9,8},{10,9... | collective-permute-start | bytes 24584 | tf_op jit(solution)/shard_map/ppermute | solution.py:290
  13.6 0.0 collective-permute-start.3
  13.6 1.4 %collective-permute-done.2.from_e = f32[16,128]{1,0:T(8,128)S(1)} collective-permute-done((f32[16,128]{1,0:T(8,128)S(1)}, f32[16,128]{1,0:T(8,128)S(1)}, u32[]{:S(2)}, u32[]{:S(2)}) %collective-permute-start.2) | collective-permute-done | bytes 8224 | tf_op jit(solution)/shard_map/ppermute | solution.py:290
  15.0 0.0 collective-permute-start.6
  15.0 2.6 %collective-permute-start.4 = (f32[16,128]{1,0:T(8,128)S(1)}, f32[16,128]{1,0:T(8,128)S(1)}, u32[]{:S(2)}, u32[]{:S(2)}) collective-permute-start(f32[16,128]{1,0:T(8,128)S(1)} %collective-permute-done.2.from_e), channel_id=1, source_target_pairs={{0,28},{4,0},{8,4},{12,8},{16,12},{20,16},{24,20},{28,24},{1,29},{... | collective-permute-start | bytes 24584 | tf_op jit(solution)/shard_map/ppermute | solution.py:294
  17.6 1.4 %collective-permute-done.3.from_w = f32[16,128]{1,0:T(8,128)S(1)} collective-permute-done((f32[16,128]{1,0:T(8,128)S(1)}, f32[16,128]{1,0:T(8,128)S(1)}, u32[]{:S(2)}, u32[]{:S(2)}) %collective-permute-start.3) | collective-permute-done | bytes 8224 | tf_op jit(solution)/shard_map/ppermute | solution.py:289
  19.1 0.0 collective-permute-start.7
  19.1 2.6 %collective-permute-start.5 = (f32[16,128]{1,0:T(8,128)S(1)}, f32[16,128]{1,0:T(8,128)S(1)}, u32[]{:S(2)}, u32[]{:S(2)}) collective-permute-start(f32[16,128]{1,0:T(8,128)S(1)} %collective-permute-done.3.from_w), channel_id=1, source_target_pairs={{0,28},{4,0},{8,4},{12,8},{16,12},{20,16},{24,20},{28,24},{1,29},{... | collective-permute-start | bytes 24584 | tf_op jit(solution)/shard_map/ppermute | solution.py:294
  21.7 0.1 pad_add_fusion.place
  21.8 0.0 collective-permute-done.4.ne
  21.8 1.2 %collective-permute-done.7.sw = f32[16,128]{1,0:T(8,128)S(1)} collective-permute-done((f32[16,128]{1,0:T(8,128)S(1)}, f32[16,128]{1,0:T(8,128)S(1)}, u32[]{:S(2)}, u32[]{:S(2)}) %collective-permute-start.7) | collective-permute-done | bytes 8224 | tf_op jit(solution)/shard_map/ppermute | solution.py:293
  23.0 0.0 collective-permute-done.5.nw
  23.1 0.0 copy-start.3
  23.1 0.8 %copy-done.3 = f32[16,640]{1,0:T(8,128)S(1)} copy-done((f32[16,640]{1,0:T(8,128)S(1)}, f32[16,640]{1,0:T(8,128)}, u32[]{:S(2)}) %copy-start.3) | copy-done | bytes 40984
  23.9 0.8 %copy-done.5 = f32[16,640]{1,0:T(8,128)S(1)} copy-done((f32[16,640]{1,0:T(8,128)S(1)}, f32[16,640]{1,0:T(8,128)}, u32[]{:S(2)}) %copy-start.5) | copy-done | bytes 40984
  24.6 0.8 %copy-done.7 = s32[16,640]{1,0:T(8,128)S(1)} copy-done((s32[16,640]{1,0:T(8,128)S(1)}, s32[16,640]{1,0:T(8,128)}, u32[]{:S(2)}) %copy-start.7) | copy-done | bytes 40984
  25.4 0.8 %copy-done.9 = f32[16,640]{1,0:T(8,128)S(1)} copy-done((f32[16,640]{1,0:T(8,128)S(1)}, f32[16,640]{1,0:T(8,128)}, u32[]{:S(2)}) %copy-start.9) | copy-done | bytes 40984
  26.2 0.8 %copy-done.11 = f32[16,640]{1,0:T(8,128)S(1)} copy-done((f32[16,640]{1,0:T(8,128)S(1)}, f32[16,640]{1,0:T(8,128)}, u32[]{:S(2)}) %copy-start.11) | copy-done | bytes 40984
  27.0 0.8 %copy-done.13 = f32[16,640]{1,0:T(8,128)S(1)} copy-done((f32[16,640]{1,0:T(8,128)S(1)}, f32[16,640]{1,0:T(8,128)}, u32[]{:S(2)}) %copy-start.13) | copy-done | bytes 40984
  27.8 16.5 %moments.1 = (f32[32,16,128]{2,1,0:T(8,128)S(1)}, f32[16,24,768]{2,1,0:T(8,128)S(1)}, f32[4,24,768]{2,1,0:T(8,128)S(1)}) custom-call(s32[2]{0:T(128)S(1)} %pad_add_fusion.place, f32[16,16,640]{2,1,0:T(8,128)S(1)} %copy-done.1, f32[16,640]{1,0:T(8,128)S(1)} %copy-done.3, f32[16,640]{1,0:T(8,128)S(1)} %copy-done.5, s32[16,640]{1,0:T(8,128)S(1)} %copy-done.7, ...), custom_call_target="tpu_custom_call" | custom-call | tf_op jit(solution)/shard_map/moments/pallas_call | solution.py:264
  44.3 15.1 %all_to_all.5.parts = f32[32,16,128]{2,1,0:T(8,128)S(1)} all-to-all(f32[32,16,128]{2,1,0:T(8,128)S(1)} %get-tuple-element.13), channel_id=1, replica_groups=mesh['lat'=8,'lon'=4] {'lat','lon'}, dimensions={0} | all-to-all | bytes 524288 | tf_op jit(solution)/shard_map/all_to_all | solution.py:307
  59.4 3.2 %finish.1 = (f32[16,640]{1,0:T(8,128)}, f32[16,640]{1,0:T(8,128)}) custom-call(f32[32,16,128]{2,1,0:T(8,128)S(1)} %all_to_all.5.parts, f32[16,640]{1,0:T(8,128)S(1)} %copy-done.3, f32[16,24,768]{2,1,0:T(8,128)S(1)} %get-tuple-element.14.basis_ext, f32[4,24,768]{2,1,0:T(8,128)S(1)} %get-tuple-element.15.side_ext), custom_call_target="tpu_custom_call" | custom-call | tf_op jit(solution)/shard_map/finish/pallas_call | solution.py:264
  (17 shorter events, 0.0 us)
Async XLA Ops:
  0.6 1.1 %copy-start = (f32[16,16,640]{2,1,0:T(8,128)S(1)}, f32[16,16,640]{2,1,0:T(8,128)}, u32[]{:S(2)}) copy-start(f32[16,16,640]{2,1,0:T(8,128)} %basis.3) | copy-start | bytes 1966084
  1.7 0.8 %copy-start.2 = (f32[16,640]{1,0:T(8,128)S(1)}, f32[16,640]{1,0:T(8,128)}, u32[]{:S(2)}) copy-start(f32[16,640]{1,0:T(8,128)} %guess.5) | copy-start | bytes 122884
  2.5 0.8 %copy-start.4 = (f32[16,640]{1,0:T(8,128)S(1)}, f32[16,640]{1,0:T(8,128)}, u32[]{:S(2)}) copy-start(f32[16,640]{1,0:T(8,128)} %rhs.3) | copy-start | bytes 122884
  3.3 0.8 %copy-start.6 = (s32[16,640]{1,0:T(8,128)S(1)}, s32[16,640]{1,0:T(8,128)}, u32[]{:S(2)}) copy-start(s32[16,640]{1,0:T(8,128)} %mask.3) | copy-start | bytes 122884
  4.1 0.8 %copy-start.8 = (f32[16,640]{1,0:T(8,128)S(1)}, f32[16,640]{1,0:T(8,128)}, u32[]{:S(2)}) copy-start(f32[16,640]{1,0:T(8,128)} %east.3) | copy-start | bytes 122884
  4.8 0.8 %copy-start.10 = (f32[16,640]{1,0:T(8,128)S(1)}, f32[16,640]{1,0:T(8,128)}, u32[]{:S(2)}) copy-start(f32[16,640]{1,0:T(8,128)} %north.3) | copy-start | bytes 122884
  5.6 0.8 %copy-start.12 = (f32[16,640]{1,0:T(8,128)S(1)}, f32[16,640]{1,0:T(8,128)}, u32[]{:S(2)}) copy-start(f32[16,640]{1,0:T(8,128)} %surf.3) | copy-start | bytes 122884
  6.4 16.7 %copy-start.1 = (f32[16,16,640]{2,1,0:T(8,128)S(1)}, f32[16,16,640]{2,1,0:T(8,128)}, u32[]{:S(2)}) copy-start(f32[16,16,640]{2,1,0:T(8,128)} %basis.3) | copy-start | bytes 1966084
  6.6 16.5 %collective-permute-start = (f32[88,640]{1,0:T(8,128)S(1)}, f32[88,640]{1,0:T(8,128)S(1)}, u32[]{:S(2)}, u32[]{:S(2)}) collective-permute-start(f32[88,640]{1,0:T(8,128)S(1)} %get-tuple-element.9), channel_id=1, source_target_pairs={{0,28},{4,0},{8,4},{12,8},{16,12},{20,16},{24,20},{28,24},{1,29},{... | collective-permute-start | bytes 675848 | tf_op jit(solution)/shard_map/ppermute | solution.py:292
  10.0 13.1 %collective-permute-start.1 = (f32[88,640]{1,0:T(8,128)S(1)}, f32[88,640]{1,0:T(8,128)S(1)}, u32[]{:S(2)}, u32[]{:S(2)}) collective-permute-start(f32[88,640]{1,0:T(8,128)S(1)} %get-tuple-element.10), channel_id=1, source_target_pairs={{0,4},{4,8},{8,12},{12,16},{16,20},{20,24},{24,28},{28,0},{1,5},{5... | collective-permute-start | bytes 675848 | tf_op jit(solution)/shard_map/ppermute | solution.py:291
  10.0 5.0 %collective-permute-start.2 = (f32[16,128]{1,0:T(8,128)S(1)}, f32[16,128]{1,0:T(8,128)S(1)}, u32[]{:S(2)}, u32[]{:S(2)}) collective-permute-start(f32[16,128]{1,0:T(8,128)S(1)} %get-tuple-element.11), channel_id=1, source_target_pairs={{0,3},{1,0},{2,1},{3,2},{4,7},{5,4},{6,5},{7,6},{8,11},{9,8},{10,9... | collective-permute-start | bytes 24584 | tf_op jit(solution)/shard_map/ppermute | solution.py:290
  13.6 5.4 %collective-permute-start.3 = (f32[16,128]{1,0:T(8,128)S(1)}, f32[16,128]{1,0:T(8,128)S(1)}, u32[]{:S(2)}, u32[]{:S(2)}) collective-permute-start(f32[16,128]{1,0:T(8,128)S(1)} %get-tuple-element.12), channel_id=1, source_target_pairs={{0,1},{1,2},{2,3},{3,0},{4,5},{5,6},{6,7},{7,4},{8,9},{9,10},{10,1... | collective-permute-start | bytes 24584 | tf_op jit(solution)/shard_map/ppermute | solution.py:289
  15.0 4.1 %collective-permute-start.6 = (f32[16,128]{1,0:T(8,128)S(1)}, f32[16,128]{1,0:T(8,128)S(1)}, u32[]{:S(2)}, u32[]{:S(2)}) collective-permute-start(f32[16,128]{1,0:T(8,128)S(1)} %collective-permute-done.2.from_e), channel_id=1, source_target_pairs={{0,4},{4,8},{8,12},{12,16},{16,20},{20,24},{24,28},{28,0},{1,5},{5... | collective-permute-start | bytes 24584 | tf_op jit(solution)/shard_map/ppermute | solution.py:293
  15.0 6.8 %collective-permute-start.4 = (f32[16,128]{1,0:T(8,128)S(1)}, f32[16,128]{1,0:T(8,128)S(1)}, u32[]{:S(2)}, u32[]{:S(2)}) collective-permute-start(f32[16,128]{1,0:T(8,128)S(1)} %collective-permute-done.2.from_e), channel_id=1, source_target_pairs={{0,28},{4,0},{8,4},{12,8},{16,12},{20,16},{24,20},{28,24},{1,29},{... | collective-permute-start | bytes 24584 | tf_op jit(solution)/shard_map/ppermute | solution.py:294
  19.1 4.0 %collective-permute-start.7 = (f32[16,128]{1,0:T(8,128)S(1)}, f32[16,128]{1,0:T(8,128)S(1)}, u32[]{:S(2)}, u32[]{:S(2)}) collective-permute-start(f32[16,128]{1,0:T(8,128)S(1)} %collective-permute-done.3.from_w), channel_id=1, source_target_pairs={{0,4},{4,8},{8,12},{12,16},{16,20},{20,24},{24,28},{28,0},{1,5},{5... | collective-permute-start | bytes 24584 | tf_op jit(solution)/shard_map/ppermute | solution.py:293
  19.1 4.0 %collective-permute-start.5 = (f32[16,128]{1,0:T(8,128)S(1)}, f32[16,128]{1,0:T(8,128)S(1)}, u32[]{:S(2)}, u32[]{:S(2)}) collective-permute-start(f32[16,128]{1,0:T(8,128)S(1)} %collective-permute-done.3.from_w), channel_id=1, source_target_pairs={{0,28},{4,0},{8,4},{12,8},{16,12},{20,16},{24,20},{28,24},{1,29},{... | collective-permute-start | bytes 24584 | tf_op jit(solution)/shard_map/ppermute | solution.py:294
  23.1 0.8 %copy-start.3 = (f32[16,640]{1,0:T(8,128)S(1)}, f32[16,640]{1,0:T(8,128)}, u32[]{:S(2)}) copy-start(f32[16,640]{1,0:T(8,128)} %guess.5) | copy-start | bytes 122884
  23.9 0.8 %copy-start.5 = (f32[16,640]{1,0:T(8,128)S(1)}, f32[16,640]{1,0:T(8,128)}, u32[]{:S(2)}) copy-start(f32[16,640]{1,0:T(8,128)} %rhs.3) | copy-start | bytes 122884
  24.6 0.8 %copy-start.7 = (s32[16,640]{1,0:T(8,128)S(1)}, s32[16,640]{1,0:T(8,128)}, u32[]{:S(2)}) copy-start(s32[16,640]{1,0:T(8,128)} %mask.3) | copy-start | bytes 122884
  25.4 0.8 %copy-start.9 = (f32[16,640]{1,0:T(8,128)S(1)}, f32[16,640]{1,0:T(8,128)}, u32[]{:S(2)}) copy-start(f32[16,640]{1,0:T(8,128)} %east.3) | copy-start | bytes 122884
  26.2 0.8 %copy-start.11 = (f32[16,640]{1,0:T(8,128)S(1)}, f32[16,640]{1,0:T(8,128)}, u32[]{:S(2)}) copy-start(f32[16,640]{1,0:T(8,128)} %north.3) | copy-start | bytes 122884
  27.0 0.8 %copy-start.13 = (f32[16,640]{1,0:T(8,128)S(1)}, f32[16,640]{1,0:T(8,128)}, u32[]{:S(2)}) copy-start(f32[16,640]{1,0:T(8,128)} %surf.3) | copy-start | bytes 122884

commit v2 on v1

--- a/solution.py
+++ b/solution.py
@@ -17,9 +17,21 @@
     return [(i, (i + step) % count) for i in range(count)]
 
 
-def pack_kernel(basis, guess, rhs, mask, east, north, surf, to_n, to_s, to_e, to_w):
+def pack_kernel(
+    basis_hbm, guess_hbm, rhs_hbm, mask_hbm, east_hbm, north_hbm, surf_hbm,
+    basis, sides, mask, to_n, to_s, to_e, to_w, sems,
+):
     vectors, rows, cols = basis.shape
-    fields = [basis.at[k] for k in range(vectors)] + [guess, rhs, mask, east, north, surf]
+    moves = [(basis_hbm, basis), (mask_hbm, mask)]
+    sources = (guess_hbm, rhs_hbm, east_hbm, north_hbm, surf_hbm)
+    moves += [(source, sides.at[i]) for i, source in enumerate(sources)]
+    copies = [pltpu.make_async_copy(a, b, sems.at[i]) for i, (a, b) in enumerate(moves)]
+    for copy in copies:
+        copy.start()
+    for copy in copies:
+        copy.wait()
+    fields = [basis.at[k] for k in range(vectors)]
+    fields += [sides.at[0], sides.at[1], mask, sides.at[2], sides.at[3], sides.at[4]]
     strip_e = jnp.zeros((rows, LANES), jnp.float32)
     strip_w = jnp.zeros((rows, LANES), jnp.float32)
     lane = lax.broadcasted_iota(jnp.int32, (rows, LANES), 1)
@@ -51,31 +63,41 @@
 
 
 def moments_kernel(
-    place, basis, guess, rhs, mask, east, north, surf,
-    from_n, from_s, from_e, from_w, ne, nw, se, sw,
-    copies, basis_ext, side_ext, powers, fields_ext,
+    place, basis, sides, mask,
+    from_n, from_s, from_e, from_w, corner_n, corner_s,
+    copies, basis_ext, side_ext, powers, fields_ext, faces, start_powers,
 ):
     vectors, rows, cols = basis.shape
     wide = cols + LANES
     tall = rows + 2 * DEPTH
+    tiles = cols // LANES
     lane = lax.broadcasted_iota(jnp.int32, (tall, LANES), 1)
-    strip_e = jnp.concatenate([from_e[...], ne[:DEPTH, :], se[rows - DEPTH :, :]], axis=0)
-    strip_w = jnp.concatenate([from_w[...], nw[:DEPTH, :], sw[rows - DEPTH :, :]], axis=0)
-
-    def extend(f, own, out):
+    strip_e = [from_e[...], corner_n[:DEPTH, :], corner_s[rows - DEPTH : rows, :]]
+    strip_w = [from_w[...], corner_n[rows : rows + DEPTH, :], corner_s[2 * rows - DEPTH :, :]]
+    strip_e = jnp.concatenate(strip_e, axis=0)
+    strip_w = jnp.concatenate(strip_w, axis=0)
+
+    def edge_of(f):
         at = DEPTH * f
-        out[:rows, :cols] = own.astype(jnp.float32)
-        out[rows : rows + DEPTH, :cols] = from_n[pl.ds(at, DEPTH), :]
-        out[rows + DEPTH :, :cols] = from_s[pl.ds(at, DEPTH), :]
         edge_e = pltpu.roll(strip_e, (-at) % LANES, 1)
         edge_w = pltpu.roll(strip_w, (LANES - DEPTH - at) % LANES, 1)
-        edge = jnp.where(lane < DEPTH, edge_e, jnp.where(lane >= LANES - DEPTH, edge_w, 0.0))
-        out[:, cols:] = edge
+        return jnp.where(lane < DEPTH, edge_e, jnp.where(lane >= LANES - DEPTH, edge_w, 0.0))
 
     for k in range(vectors):
-        extend(k, basis[k], basis_ext.at[k])
-    for f, ref in enumerate((guess, rhs, mask, east, north, surf)):
-        extend(vectors + f, ref[...], fields_ext.at[f])
+        at, to = DEPTH * k, tall * k
+        for tile in range(tiles):
+            part = pl.ds(tile * LANES, LANES)
+            basis_ext[tile, pl.ds(to, rows), :] = basis[k, :, part]
+            basis_ext[tile, pl.ds(to + rows, DEPTH), :] = from_n[pl.ds(at, DEPTH), part]
+            basis_ext[tile, pl.ds(to + rows + DEPTH, DEPTH), :] = from_s[pl.ds(at, DEPTH), part]
+        basis_ext[tiles, pl.ds(to, tall), :] = edge_of(k)
+    own = (sides.at[0], sides.at[1], mask, sides.at[2], sides.at[3], sides.at[4])
+    for f, ref in enumerate(own):
+        at = DEPTH * (vectors + f)
+        fields_ext[f, :rows, :cols] = ref[...].astype(jnp.float32)
+        fields_ext[f, rows : rows + DEPTH, :cols] = from_n[pl.ds(at, DEPTH), :]
+        fields_ext[f, rows + DEPTH :, :cols] = from_s[pl.ds(at, DEPTH), :]
+        fields_ext[f, :, cols:] = edge_of(vectors + f)
     row = lax.broadcasted_iota(jnp.int32, (tall, wide), 0)
     beyond_n = (row >= rows) & (row < rows + DEPTH) & (place[0] == place[1] - 1)
     beyond_s = (row >= rows + DEPTH) & (place[0] == 0)
@@ -88,43 +110,67 @@
     side_ext[2] = k_north
     start = fields_ext[1] - apply_faces(fields_ext[0], diag, k_east, k_north)
     side_ext[3] = start
-
-    def put(index, v):
-        for tile in range(cols // LANES):
-            at = tile * LANES
-            powers[tile, pl.ds(index * rows, rows), :] = v[:rows, at : at + LANES]
-
-    def shifted(v):
-        return apply_faces(v, side_ext[0] - SHIFT, side_ext[1], side_ext[2])
-
-    def one_vector(k, carry):
-        v = basis_ext[k]
-        put(k, v)
-        v = apply_faces(v, side_ext[0], side_ext[1], side_ext[2])
-        put(vectors + k, v)
-        for power in range(ITERS):
-            v = shifted(v)
-            put((2 + power) * vectors + k, v)
-        return carry
-
-    lax.fori_loop(0, vectors, one_vector, 0)
     v = start
+    for power in range(ITERS + 1):
+        for tile in range(tiles):
+            part = v[:rows, tile * LANES : (tile + 1) * LANES]
+            start_powers[tile, pl.ds(power * rows, rows), :] = part
+        if power < ITERS:
+            v = apply_faces(v, side_ext[0] - SHIFT, side_ext[1], side_ext[2])
+    spare = (8 - (ITERS + 1)) * rows
+    start_powers[:, pl.ds((ITERS + 1) * rows, spare), :] = jnp.zeros(
+        (tiles, spare, LANES), jnp.float32
+    )
+
+    for q in range(tall):
+        ring_row = (q - DEPTH) % tall
+        for c, coeff in enumerate((side_ext.at[0], side_ext.at[1], side_ext.at[2])):
+            spread = jnp.broadcast_to(coeff[ring_row : ring_row + 1, :], (8, wide))
+            faces[c, q] = spread
+            if c == 0:
+                faces[3, q] = spread - SHIFT
+        for tile in range(tiles + 1):
+            part = basis_ext[tile, pl.ds(ring_row, vectors, stride=tall), :]
+            powers[q, :vectors, tile * LANES : (tile + 1) * LANES] = part
+
+    def coefficient(c, q):
+        return jnp.concatenate([faces[c, q]] * (vectors // 8), axis=0)
+
+    unroll = 2
+    for power in range(DEPTH):
+        first, last = 1 + power, tall - 1 - power
+        source = slice(power * vectors, (power + 1) * vectors)
+        target = slice((power + 1) * vectors, (power + 2) * vectors)
+        middle = 0 if power == 0 else 3
+
+        def some_rows(i, flux_s, first=first, source=source, target=target, middle=middle):
+            for u in range(unroll):
+                q = first + i * unroll + u
+                v = powers[q, source, :]
+                flux_n = coefficient(2, q) * (v - powers[q + 1, source, :])
+                flux_e = coefficient(1, q) * (v - roll_lanes(v, -1))
+                image = coefficient(middle, q) * v + (flux_e - roll_lanes(flux_e, 1))
+                powers[q, target, :] = image + (flux_n - flux_s)
+                flux_s = flux_n
+            return flux_s
+
+        below = first - 1
+        flux = powers[below, source, :] - powers[first, source, :]
+        lax.fori_loop(0, (last - first) // unroll, some_rows, coefficient(2, below) * flux)
+
     base = (ITERS + 2) * vectors
-    put(base, v)
-    for power in range(ITERS):
-        v = shifted(v)
-        put(base + 1 + power, v)
-    spare = 8 - (ITERS + 1)
-    powers[:, pl.ds((base + ITERS + 1) * rows, spare * rows), :] = jnp.zeros(
-        (cols // LANES, spare * rows, LANES), jnp.float32
-    )
     count = base + 8
+    batch = 4
     nt = (((1,), (1,)), ((), ()))
 
-    def one_row(r, carry):
+    def one_batch(i, carry):
         high_sum, cross_sum = carry
-        tiles = range(cols // LANES)
-        x = [powers[tile, pl.ds(r, count, stride=rows), :] for tile in tiles]
+        x = []
+        for u in range(batch):
+            r = i * batch + u
+            tail = [start_powers[t, pl.ds(r, 8, stride=rows), :] for t in range(tiles)]
+            tail = jnp.concatenate(tail, axis=1)
+            x.append(jnp.concatenate([powers[r + DEPTH, :, :cols], tail], axis=0))
         x = jnp.concatenate(x, axis=1)
         high = x.astype(jnp.bfloat16)
         low = (x - high.astype(jnp.float32)).astype(jnp.bfloat16)
@@ -133,7 +179,7 @@
         return high_sum, cross_sum
 
     zero = jnp.zeros((count, count), jnp.float32)
-    high_sum, cross_sum = lax.fori_loop(0, rows, one_row, (zero, zero))
+    high_sum, cross_sum = lax.fori_loop(0, rows // batch, one_batch, (zero, zero))
     full = high_sum + cross_sum + cross_sum.T
     full = jnp.concatenate([full, jnp.zeros((count, LANES - count), jnp.float32)], axis=1)
     at = lax.broadcasted_iota(jnp.int32, (vectors, LANES), 1)
@@ -163,9 +209,10 @@
     lax.fori_loop(0, copies.shape[0], one_copy, 0, unroll=8)
 
 
-def finish_kernel(parts, guess, basis_ext, side_ext, solution, residual, spread):
-    vectors, tall, wide = basis_ext.shape
-    rows, cols = guess.shape
+def finish_kernel(parts, sides, basis_ext, side_ext, solution, residual, spread):
+    _, tall, wide = side_ext.shape
+    _, rows, cols = sides.shape
+    vectors = basis_ext.shape[1] // tall
     free = 7 * vectors
     several = 8
 
@@ -239,7 +286,7 @@
     for tile in range(wide // LANES):
         acc = [jnp.zeros((tall, LANES), jnp.float32) for _ in range(ITERS + 1)]
         for k in range(vectors):
-            w = basis_ext[k, :, pl.ds(tile * LANES, LANES)]
+            w = basis_ext[tile, pl.ds(tall * k, tall), :]
             for i in range(ITERS + 1):
                 acc[i] = acc[i] + w * spread[i, pl.ds(k, 1), :]
         for i in range(ITERS + 1):
@@ -248,7 +295,7 @@
     diag, k_east, k_north = side_ext[0], side_ext[1], side_ext[2]
     image = functools.partial(apply_faces, k_east=k_east, k_north=k_north)
     v = side_ext[3] + image(along[0], diag)
-    x = guess[...] - along[0][:rows, :cols]
+    x = sides[0] - along[0][:rows, :cols]
     r = rho[0] * v[:rows, :cols]
     for i in range(ITERS):
         x = x + delta[i] * (v + along[i + 1])[:rows, :cols]
@@ -258,13 +305,11 @@
     residual[...] = r
 
 
-def call(kernel, out_shape, inputs, scratch=(), smem=0, name=None):
-    specs = [pl.BlockSpec(memory_space=pltpu.SMEM)] * smem
-    specs += [pl.BlockSpec(memory_space=pltpu.VMEM)] * (len(inputs) - smem)
+def call(kernel, out_shape, spaces, inputs, scratch=(), name=None):
     return pl.pallas_call(
         kernel,
         out_shape=out_shape,
-        in_specs=specs,
+        in_specs=[pl.BlockSpec(memory_space=space) for space in spaces],
         out_specs=[pl.BlockSpec(memory_space=pltpu.VMEM)] * len(out_shape),
         scratch_shapes=scratch,
         name=name,
@@ -282,33 +327,46 @@
     devices = n_lat * n_lon
     fields = vectors + 6
     tall, wide = rows + 2 * DEPTH, cols + LANES
+    tiles = cols // LANES
     own = (recycled, first_guess, right_side, cell_mask, cond_east, cond_north, surface)
     band, strip = f32(fields * DEPTH, cols), f32(rows, LANES)
-    to_n, to_s, to_e, to_w = call(pack_kernel, [band, band, strip, strip], own, name="pack")
+    basis, sides, mask, to_n, to_s, to_e, to_w = call(
+        pack_kernel,
+        [f32(vectors, rows, cols), f32(5, rows, cols), jax.ShapeDtypeStruct((rows, cols), jnp.int32)]
+        + [band, band, strip, strip],
+        [pltpu.HBM] * 7,
+        own,
+        scratch=[pltpu.SemaphoreType.DMA((7,))],
+        name="pack",
+    )
     north, south = ring(n_lat, 1), ring(n_lat, -1)
     from_w = lax.ppermute(to_e, "lon", ring(n_lon, 1))
     from_e = lax.ppermute(to_w, "lon", ring(n_lon, -1))
     from_s = lax.ppermute(to_n, "lat", north)
     from_n = lax.ppermute(to_s, "lat", south)
-    se, sw = lax.ppermute(from_e, "lat", north), lax.ppermute(from_w, "lat", north)
-    ne, nw = lax.ppermute(from_e, "lat", south), lax.ppermute(from_w, "lat", south)
+    strips = jnp.concatenate([from_e, from_w], axis=0)
+    corner_s = lax.ppermute(strips, "lat", north)
+    corner_n = lax.ppermute(strips, "lat", south)
     place = jnp.stack([lax.axis_index("lat"), jnp.int32(n_lat)])
     copies, basis_ext, side_ext = call(
         moments_kernel,
-        [f32(devices, vectors, LANES), f32(vectors, tall, wide), f32(4, tall, wide)],
-        (place,) + own + (from_n, from_s, from_e, from_w, ne, nw, se, sw),
+        [f32(devices, vectors, LANES), f32(tiles + 1, vectors * tall, LANES), f32(4, tall, wide)],
+        [pltpu.SMEM] + [pltpu.VMEM] * 9,
+        (place, basis, sides, mask, from_n, from_s, from_e, from_w, corner_n, corner_s),
         scratch=[
-            pltpu.VMEM((cols // LANES, ((ITERS + 2) * vectors + 8) * rows, LANES), jnp.float32),
+            pltpu.VMEM((tall, (ITERS + 2) * vectors, wide), jnp.float32),
             pltpu.VMEM((6, tall, wide), jnp.float32),
+            pltpu.VMEM((4, tall, 8, wide), jnp.float32),
+            pltpu.VMEM((tiles, 8 * rows, LANES), jnp.float32),
         ],
-        smem=1,
         name="moments",
     )
     parts = lax.all_to_all(copies, ("lat", "lon"), 0, 0)
     return call(
         finish_kernel,
         [f32(rows, cols), f32(rows, cols)],
-        (parts, first_guess, basis_ext, side_ext),
+        [pltpu.VMEM] * 4,
+        (parts, sides, basis_ext, side_ext),
         scratch=[pltpu.VMEM((ITERS + 1, vectors, LANES), jnp.float32)],
         name="finish",
     )

time: 63.4 us -> 49.6 us (0.78)
  Pallas kernels: 19.9 us -> 13.9 us
  local copies, waits for them, and re-layouts: 10.4 us -> 5.75 us
  starting transfers between devices: 12.3 us -> 9.39 us
  waiting for transfers between devices: 4.1 us -> 5.2 us
  blocking collectives: 15.1 us -> 14.1 us
    pallas_call x3, Pallas kernels: 19.9 us -> 13.9 us  [call(): pl.pallas_call(kernel, out_shape=out_shape, in_specs=[pl.BlockSpec(memory...]
    unnamed x28 -> x15, local copies, waits for them, and re-layouts: 10.4 us -> 5.75 us
    ppermute x4 -> x2, starting transfers between devices: 5.29 us -> 2.64 us  [the longest x1 2.64 us: shards(): corner_n = lax.ppermute(strips, 'lat', south)]
    ppermute x1, waiting for transfers between devices: 1.44 us -> 3.83 us  [shards(): from_w = lax.ppermute(to_e, 'lon', ring(n_lon, 1))]
    ppermute x1, starting transfers between devices: 3.41 us -> 1.61 us  [shards(): from_n = lax.ppermute(to_s, 'lat', south)]
    ppermute x1, starting transfers between devices: 3.6 us -> 5.13 us  [shards(): from_e = lax.ppermute(to_w, 'lon', ring(n_lon, -1))]
    ppermute x1, waiting for transfers between devices: 1.36 us -> 0.01 us  [shards(): from_e = lax.ppermute(to_w, 'lon', ring(n_lon, -1))]
    all_to_all x1, blocking collectives: 15.1 us -> 14.1 us  [shards(): parts = lax.all_to_all(copies, ('lat', 'lon'), 0, 0)]
  transfers between devices with their start and end apart: 8 -> 6, of which waited for: 3 -> 2; matrix products, arithmetic and copies ran while one was open for 0% -> 0% of each run, Pallas kernels for 0% -> 0%
where the time goes in v2:
time: 49.6 us; the launch traced here: 49.1 us
  blocking collectives  14.1 us (28%)
  Pallas kernels  13.9 us (28%)
  starting transfers between devices  9.39 us (19%)
  local copies, waits for them, and re-layouts  5.75 us (12%)
  waiting for transfers between devices  5.2 us (10%)
  between operations  0.67 us (1%)
    all_to_all x1, blocking collectives, shards(): parts = lax.all_to_all(copies, ('lat', 'lon'), 0, 0)  14.1 us
    pallas_call x3, Pallas kernels, call(): pl.pallas_call(kernel, out_shape=out_shape, in_specs=[pl.BlockSpec(memory...  13.9 us
    unnamed x15, local copies, waits for them, and re-layouts  5.75 us
    ppermute x1, starting transfers between devices, shards(): from_e = lax.ppermute(to_w, 'lon', ring(n_lon, -1))  5.13 us
    ppermute x1, waiting for transfers between devices, shards(): from_w = lax.ppermute(to_e, 'lon', ring(n_lon, 1))  3.83 us
    ppermute x1, starting transfers between devices, shards(): corner_n = lax.ppermute(strips, 'lat', south)  2.64 us
    ppermute x1, starting transfers between devices, shards(): from_n = lax.ppermute(to_s, 'lat', south)  1.61 us
    ppermute x1, waiting for transfers between devices, shards(): corner_s = lax.ppermute(strips, 'lat', north)  1.34 us
  transfers between devices with their start and end apart: 6, of which 2 were waited for; matrix products, arithmetic and copies ran while one was open for 0% of the time, Pallas kernels for 0%

profile of v2, /device:TPU:0, one launch (start us, length us, event | category | flops | bytes accessed | tf_op | source)
XLA Modules:
  0.0 49.1 jit_solution(14614238871652042619)
XLA Ops:
  0.6 0.0 copy-start
  0.6 1.1 %copy-done = f32[16,16,640]{2,1,0:T(8,128)S(1)} copy-done((f32[16,16,640]{2,1,0:T(8,128)S(1)}, f32[16,16,640]{2,1,0:T(8,128)}, u32[]{:S(2)}) %copy-start) | copy-done | bytes 655384
  1.7 0.0 copy-start.1
  1.7 0.8 %copy-done.1 = f32[16,640]{1,0:T(8,128)S(1)} copy-done((f32[16,640]{1,0:T(8,128)S(1)}, f32[16,640]{1,0:T(8,128)}, u32[]{:S(2)}) %copy-start.1) | copy-done | bytes 40984
  2.5 0.0 copy-start.2
  2.5 0.8 %copy-done.2 = f32[16,640]{1,0:T(8,128)S(1)} copy-done((f32[16,640]{1,0:T(8,128)S(1)}, f32[16,640]{1,0:T(8,128)}, u32[]{:S(2)}) %copy-start.2) | copy-done | bytes 40984
  3.3 0.0 copy-start.3
  3.3 0.8 %copy-done.3 = s32[16,640]{1,0:T(8,128)S(1)} copy-done((s32[16,640]{1,0:T(8,128)S(1)}, s32[16,640]{1,0:T(8,128)}, u32[]{:S(2)}) %copy-start.3) | copy-done | bytes 40984
  4.1 0.0 copy-start.4
  4.1 0.8 %copy-done.4 = f32[16,640]{1,0:T(8,128)S(1)} copy-done((f32[16,640]{1,0:T(8,128)S(1)}, f32[16,640]{1,0:T(8,128)}, u32[]{:S(2)}) %copy-start.4) | copy-done | bytes 40984
  4.8 0.0 copy-start.5
  4.8 0.8 %copy-done.5 = f32[16,640]{1,0:T(8,128)S(1)} copy-done((f32[16,640]{1,0:T(8,128)S(1)}, f32[16,640]{1,0:T(8,128)}, u32[]{:S(2)}) %copy-start.5) | copy-done | bytes 40984
  5.6 0.0 copy-start.6
  5.6 0.8 %copy-done.6 = f32[16,640]{1,0:T(8,128)S(1)} copy-done((f32[16,640]{1,0:T(8,128)S(1)}, f32[16,640]{1,0:T(8,128)}, u32[]{:S(2)}) %copy-start.6) | copy-done | bytes 40984
  6.4 0.8 %pack.1 = (f32[16,16,640]{2,1,0:T(8,128)S(1)}, f32[5,16,640]{2,1,0:T(8,128)S(1)}, s32[16,640]{1,0:T(8,128)S(1)}, f32[88,640]{1,0:T(8,128)S(1)}, f32[88,640]{1,0:...) custom-call(f32[16,16,640]{2,1,0:T(8,128)S(1)} %copy-done, f32[16,640]{1,0:T(8,128)S(1)} %copy-done.1, ...), custom_call_target="tpu_custom_call" | custom-call | tf_op jit(solution)/shard_map/pack/pallas_call | solution.py:309
  7.2 5.1 %collective-permute-start.2 = (f32[16,128]{1,0:T(8,128)S(1)}, f32[16,128]{1,0:T(8,128)S(1)}, u32[]{:S(2)}, u32[]{:S(2)}) collective-permute-start(f32[16,128]{1,0:T(8,128)S(1)} %get-tuple-element.17), channel_id=1, source_target_pairs={{0,3},{1,0},{2,1},{3,2},{4,7},{5,4},{6,5},{7,6},{8,11},{9,8},{10,9... | collective-permute-start | bytes 24584 | tf_op jit(solution)/shard_map/ppermute | solution.py:344
  12.4 0.0 collective-permute-start.3
  12.4 1.6 %collective-permute-start = (f32[88,640]{1,0:T(8,128)S(1)}, f32[88,640]{1,0:T(8,128)S(1)}, u32[]{:S(2)}, u32[]{:S(2)}) collective-permute-start(f32[88,640]{1,0:T(8,128)S(1)} %get-tuple-element.15), channel_id=1, source_target_pairs={{0,28},{4,0},{8,4},{12,8},{16,12},{20,16},{24,20},{28,24},{1,29},{... | collective-permute-start | bytes 675848 | tf_op jit(solution)/shard_map/ppermute | solution.py:346
  14.0 0.0 collective-permute-start.1
  14.0 0.0 collective-permute-done.2.from_e
  14.0 3.8 %collective-permute-done.3.from_w = f32[16,128]{1,0:T(8,128)S(1)} collective-permute-done((f32[16,128]{1,0:T(8,128)S(1)}, f32[16,128]{1,0:T(8,128)S(1)}, u32[]{:S(2)}, u32[]{:S(2)}) %collective-permute-start.3) | collective-permute-done | bytes 8224 | tf_op jit(solution)/shard_map/ppermute | solution.py:343
  17.8 0.0 collective-permute-start.5
  17.8 2.6 %collective-permute-start.4 = (f32[32,128]{1,0:T(8,128)S(1)}, f32[32,128]{1,0:T(8,128)S(1)}, u32[]{:S(2)}, u32[]{:S(2)}) collective-permute-start(f32[32,128]{1,0:T(8,128)S(1)} %constant_dynamic-update-slice_fusion), channel_id=1, source_target_pairs={{0,28},{4,0},{8,4},{12,8},{16,12},{20,16},{24,20},{28,24},{1,29},{... | collective-permute-start | bytes 49160 | tf_op jit(solution)/shard_map/ppermute | solution.py:349
  20.5 0.1 pad_add_fusion.place
  20.5 1.3 %collective-permute-done.5.corner_s = f32[32,128]{1,0:T(8,128)S(1)} collective-permute-done((f32[32,128]{1,0:T(8,128)S(1)}, f32[32,128]{1,0:T(8,128)S(1)}, u32[]{:S(2)}, u32[]{:S(2)}) %collective-permute-start.5) | collective-permute-done | bytes 16416 | tf_op jit(solution)/shard_map/ppermute | solution.py:348
  21.9 0.0 collective-permute-done.4.corner_n
  21.9 0.0 collective-permute-done.from_n
  21.9 0.0 collective-permute-done.1.from_s
  21.9 9.9 %moments.1 = (f32[32,16,128]{2,1,0:T(8,128)S(1)}, f32[6,384,128]{2,1,0:T(8,128)S(1)}, f32[4,24,768]{2,1,0:T(8,128)S(1)}) custom-call(s32[2]{0:T(128)S(1)} %pad_add_fusion.place, f32[16,16,640]{2,1,0:T(8,128)S(1)} %get-tuple-element.12.basis, f32[5,16,640]{2,1,0:T(8,128)S(1)} %get-tuple-element.13.sides, s32[16,640]{1,0:T(8,128)S(1)} %get-tuple-element.14.mask, ...), custom_call_target="tpu_custom_call" | custom-call | tf_op jit(solution)/shard_map/moments/pallas_call | solution.py:309
  31.8 14.1 %all_to_all.5.parts = f32[32,16,128]{2,1,0:T(8,128)S(1)} all-to-all(f32[32,16,128]{2,1,0:T(8,128)S(1)} %get-tuple-element.19), channel_id=1, replica_groups=mesh['lat'=8,'lon'=4] {'lat','lon'}, dimensions={0} | all-to-all | bytes 524288 | tf_op jit(solution)/shard_map/all_to_all | solution.py:364
  45.9 3.2 %finish.1 = (f32[16,640]{1,0:T(8,128)}, f32[16,640]{1,0:T(8,128)}) custom-call(f32[32,16,128]{2,1,0:T(8,128)S(1)} %all_to_all.5.parts, f32[5,16,640]{2,1,0:T(8,128)S(1)} %get-tuple-element.13.sides, f32[6,384,128]{2,1,0:T(8,128)S(1)} %get-tuple-element.20.basis_ext, f32[4,24,768]{2,1,0:T(8,128)S(1)} %get-tuple-element.21.side_ext), custom_call_target="tpu_custom_call" | custom-call | tf_op jit(solution)/shard_map/finish/pallas_call | solution.py:309
  (2 shorter events, 0.0 us)
Async XLA Ops:
  0.6 1.1 %copy-start = (f32[16,16,640]{2,1,0:T(8,128)S(1)}, f32[16,16,640]{2,1,0:T(8,128)}, u32[]{:S(2)}) copy-start(f32[16,16,640]{2,1,0:T(8,128)} %basis_hbm.1) | copy-start | bytes 1966084
  1.7 0.8 %copy-start.1 = (f32[16,640]{1,0:T(8,128)S(1)}, f32[16,640]{1,0:T(8,128)}, u32[]{:S(2)}) copy-start(f32[16,640]{1,0:T(8,128)} %guess_hbm.1) | copy-start | bytes 122884
  2.5 0.8 %copy-start.2 = (f32[16,640]{1,0:T(8,128)S(1)}, f32[16,640]{1,0:T(8,128)}, u32[]{:S(2)}) copy-start(f32[16,640]{1,0:T(8,128)} %rhs_hbm.1) | copy-start | bytes 122884
  3.3 0.8 %copy-start.3 = (s32[16,640]{1,0:T(8,128)S(1)}, s32[16,640]{1,0:T(8,128)}, u32[]{:S(2)}) copy-start(s32[16,640]{1,0:T(8,128)} %mask_hbm.1) | copy-start | bytes 122884
  4.1 0.8 %copy-start.4 = (f32[16,640]{1,0:T(8,128)S(1)}, f32[16,640]{1,0:T(8,128)}, u32[]{:S(2)}) copy-start(f32[16,640]{1,0:T(8,128)} %east_hbm.1) | copy-start | bytes 122884
  4.8 0.8 %copy-start.5 = (f32[16,640]{1,0:T(8,128)S(1)}, f32[16,640]{1,0:T(8,128)}, u32[]{:S(2)}) copy-start(f32[16,640]{1,0:T(8,128)} %north_hbm.1) | copy-start | bytes 122884
  5.6 0.8 %copy-start.6 = (f32[16,640]{1,0:T(8,128)S(1)}, f32[16,640]{1,0:T(8,128)}, u32[]{:S(2)}) copy-start(f32[16,640]{1,0:T(8,128)} %surf_hbm.1) | copy-start | bytes 122884
  7.2 6.7 %collective-permute-start.2 = (f32[16,128]{1,0:T(8,128)S(1)}, f32[16,128]{1,0:T(8,128)S(1)}, u32[]{:S(2)}, u32[]{:S(2)}) collective-permute-start(f32[16,128]{1,0:T(8,128)S(1)} %get-tuple-element.17), channel_id=1, source_target_pairs={{0,3},{1,0},{2,1},{3,2},{4,7},{5,4},{6,5},{7,6},{8,11},{9,8},{10,9... | collective-permute-start | bytes 24584 | tf_op jit(solution)/shard_map/ppermute | solution.py:344
  12.4 5.4 %collective-permute-start.3 = (f32[16,128]{1,0:T(8,128)S(1)}, f32[16,128]{1,0:T(8,128)S(1)}, u32[]{:S(2)}, u32[]{:S(2)}) collective-permute-start(f32[16,128]{1,0:T(8,128)S(1)} %get-tuple-element.18), channel_id=1, source_target_pairs={{0,1},{1,2},{2,3},{3,0},{4,5},{5,6},{6,7},{7,4},{8,9},{9,10},{10,1... | collective-permute-start | bytes 24584 | tf_op jit(solution)/shard_map/ppermute | solution.py:343
  12.4 9.5 %collective-permute-start = (f32[88,640]{1,0:T(8,128)S(1)}, f32[88,640]{1,0:T(8,128)S(1)}, u32[]{:S(2)}, u32[]{:S(2)}) collective-permute-start(f32[88,640]{1,0:T(8,128)S(1)} %get-tuple-element.15), channel_id=1, source_target_pairs={{0,28},{4,0},{8,4},{12,8},{16,12},{20,16},{24,20},{28,24},{1,29},{... | collective-permute-start | bytes 675848 | tf_op jit(solution)/shard_map/ppermute | solution.py:346
  14.0 7.9 %collective-permute-start.1 = (f32[88,640]{1,0:T(8,128)S(1)}, f32[88,640]{1,0:T(8,128)S(1)}, u32[]{:S(2)}, u32[]{:S(2)}) collective-permute-start(f32[88,640]{1,0:T(8,128)S(1)} %get-tuple-element.16), channel_id=1, source_target_pairs={{0,4},{4,8},{8,12},{12,16},{16,20},{20,24},{24,28},{28,0},{1,5},{5... | collective-permute-start | bytes 675848 | tf_op jit(solution)/shard_map/ppermute | solution.py:345
  17.8 4.1 %collective-permute-start.5 = (f32[32,128]{1,0:T(8,128)S(1)}, f32[32,128]{1,0:T(8,128)S(1)}, u32[]{:S(2)}, u32[]{:S(2)}) collective-permute-start(f32[32,128]{1,0:T(8,128)S(1)} %constant_dynamic-update-slice_fusion), channel_id=1, source_target_pairs={{0,4},{4,8},{8,12},{12,16},{16,20},{20,24},{24,28},{28,0},{1,5},{5... | collective-permute-start | bytes 49160 | tf_op jit(solution)/shard_map/ppermute | solution.py:348
  17.8 4.1 %collective-permute-start.4 = (f32[32,128]{1,0:T(8,128)S(1)}, f32[32,128]{1,0:T(8,128)S(1)}, u32[]{:S(2)}, u32[]{:S(2)}) collective-permute-start(f32[32,128]{1,0:T(8,128)S(1)} %constant_dynamic-update-slice_fusion), channel_id=1, source_target_pairs={{0,28},{4,0},{8,4},{12,8},{16,12},{20,16},{24,20},{28,24},{1,29},{... | collective-permute-start | bytes 49160 | tf_op jit(solution)/shard_map/ppermute | solution.py:349

commit v3 on v2

--- a/solution.py
+++ b/solution.py
@@ -335,7 +335,7 @@
         [f32(vectors, rows, cols), f32(5, rows, cols), jax.ShapeDtypeStruct((rows, cols), jnp.int32)]
         + [band, band, strip, strip],
         [pltpu.HBM] * 7,
-        own,
+        [pltpu.with_memory_space_constraint(array, pltpu.HBM) for array in own],
         scratch=[pltpu.SemaphoreType.DMA((7,))],
         name="pack",
     )

time: 49.6 us -> 44 us (0.89)
  local copies, waits for them, and re-layouts: 5.75 us -> 0.01 us
  Pallas kernels: 13.9 us -> 14.4 us
    unnamed x15 -> x1, local copies, waits for them, and re-layouts: 5.75 us -> 0.01 us
    pallas_call x3, Pallas kernels: 13.9 us -> 14.4 us  [call(): pl.pallas_call(kernel, out_shape=out_shape, in_specs=[pl.BlockSpec(memory...]
where the time goes in v3:
time: 44 us; the launch traced here: 43.9 us
  Pallas kernels  14.4 us (33%)
  blocking collectives  14.1 us (32%)
  starting transfers between devices  9.39 us (21%)
  waiting for transfers between devices  5.2 us (12%)
  between operations  0.66 us (2%)
    pallas_call x3, Pallas kernels, call(): pl.pallas_call(kernel, out_shape=out_shape, in_specs=[pl.BlockSpec(memory...  14.4 us
    all_to_all x1, blocking collectives, shards(): parts = lax.all_to_all(copies, ('lat', 'lon'), 0, 0)  14.1 us
    ppermute x1, starting transfers between devices, shards(): from_e = lax.ppermute(to_w, 'lon', ring(n_lon, -1))  5.13 us
    ppermute x1, waiting for transfers between devices, shards(): from_w = lax.ppermute(to_e, 'lon', ring(n_lon, 1))  3.83 us
    ppermute x1, starting transfers between devices, shards(): corner_n = lax.ppermute(strips, 'lat', south)  2.64 us
    ppermute x1, starting transfers between devices, shards(): from_n = lax.ppermute(to_s, 'lat', south)  1.61 us
    ppermute x1, waiting for transfers between devices, shards(): corner_s = lax.ppermute(strips, 'lat', north)  1.34 us
  transfers between devices with their start and end apart: 6, of which 2 were waited for; matrix products, arithmetic and copies ran while one was open for 0% of the time, Pallas kernels for 0%

profile of v3, /device:TPU:0, one launch (start us, length us, event | category | flops | bytes accessed | tf_op | source)
XLA Modules:
  0.0 43.9 jit_solution(4444145903188189572)
XLA Ops:
  0.6 1.4 %pack.1 = (f32[16,16,640]{2,1,0:T(8,128)S(1)}, f32[5,16,640]{2,1,0:T(8,128)S(1)}, s32[16,640]{1,0:T(8,128)S(1)}, f32[88,640]{1,0:T(8,128)S(1)}, f32[88,640]{1,0:...) custom-call(f32[16,16,640]{2,1,0:T(8,128)} %basis_hbm.1, f32[16,640]{1,0:T(8,128)} %guess_hbm.1, ...), custom_call_target="tpu_custom_call" | custom-call | tf_op jit(solution)/shard_map/pack/pallas_call | solution.py:309
  2.0 5.1 %collective-permute-start.2 = (f32[16,128]{1,0:T(8,128)S(1)}, f32[16,128]{1,0:T(8,128)S(1)}, u32[]{:S(2)}, u32[]{:S(2)}) collective-permute-start(f32[16,128]{1,0:T(8,128)S(1)} %get-tuple-element.17), channel_id=1, source_target_pairs={{0,3},{1,0},{2,1},{3,2},{4,7},{5,4},{6,5},{7,6},{8,11},{9,8},{10,9... | collective-permute-start | bytes 24584 | tf_op jit(solution)/shard_map/ppermute | solution.py:344
  7.2 0.0 collective-permute-start.3
  7.2 1.6 %collective-permute-start = (f32[88,640]{1,0:T(8,128)S(1)}, f32[88,640]{1,0:T(8,128)S(1)}, u32[]{:S(2)}, u32[]{:S(2)}) collective-permute-start(f32[88,640]{1,0:T(8,128)S(1)} %get-tuple-element.15), channel_id=1, source_target_pairs={{0,28},{4,0},{8,4},{12,8},{16,12},{20,16},{24,20},{28,24},{1,29},{... | collective-permute-start | bytes 675848 | tf_op jit(solution)/shard_map/ppermute | solution.py:346
  8.8 0.0 collective-permute-start.1
  8.8 0.0 collective-permute-done.2.from_e
  8.8 3.8 %collective-permute-done.3.from_w = f32[16,128]{1,0:T(8,128)S(1)} collective-permute-done((f32[16,128]{1,0:T(8,128)S(1)}, f32[16,128]{1,0:T(8,128)S(1)}, u32[]{:S(2)}, u32[]{:S(2)}) %collective-permute-start.3) | collective-permute-done | bytes 8224 | tf_op jit(solution)/shard_map/ppermute | solution.py:343
  12.6 0.0 collective-permute-start.5
  12.6 2.6 %collective-permute-start.4 = (f32[32,128]{1,0:T(8,128)S(1)}, f32[32,128]{1,0:T(8,128)S(1)}, u32[]{:S(2)}, u32[]{:S(2)}) collective-permute-start(f32[32,128]{1,0:T(8,128)S(1)} %constant_dynamic-update-slice_fusion), channel_id=1, source_target_pairs={{0,28},{4,0},{8,4},{12,8},{16,12},{20,16},{24,20},{28,24},{1,29},{... | collective-permute-start | bytes 49160 | tf_op jit(solution)/shard_map/ppermute | solution.py:349
  15.3 0.1 pad_add_fusion.place
  15.3 1.3 %collective-permute-done.5.corner_s = f32[32,128]{1,0:T(8,128)S(1)} collective-permute-done((f32[32,128]{1,0:T(8,128)S(1)}, f32[32,128]{1,0:T(8,128)S(1)}, u32[]{:S(2)}, u32[]{:S(2)}) %collective-permute-start.5) | collective-permute-done | bytes 16416 | tf_op jit(solution)/shard_map/ppermute | solution.py:348
  16.7 0.0 collective-permute-done.4.corner_n
  16.7 0.0 collective-permute-done.from_n
  16.7 0.0 collective-permute-done.1.from_s
  16.7 9.9 %moments.1 = (f32[32,16,128]{2,1,0:T(8,128)S(1)}, f32[6,384,128]{2,1,0:T(8,128)S(1)}, f32[4,24,768]{2,1,0:T(8,128)S(1)}) custom-call(s32[2]{0:T(128)S(1)} %pad_add_fusion.place, f32[16,16,640]{2,1,0:T(8,128)S(1)} %get-tuple-element.12.basis, f32[5,16,640]{2,1,0:T(8,128)S(1)} %get-tuple-element.13.sides, s32[16,640]{1,0:T(8,128)S(1)} %get-tuple-element.14.mask, ...), custom_call_target="tpu_custom_call" | custom-call | tf_op jit(solution)/shard_map/moments/pallas_call | solution.py:309
  26.6 14.1 %all_to_all.5.parts = f32[32,16,128]{2,1,0:T(8,128)S(1)} all-to-all(f32[32,16,128]{2,1,0:T(8,128)S(1)} %get-tuple-element.19), channel_id=1, replica_groups=mesh['lat'=8,'lon'=4] {'lat','lon'}, dimensions={0} | all-to-all | bytes 524288 | tf_op jit(solution)/shard_map/all_to_all | solution.py:364
  40.7 3.2 %finish.1 = (f32[16,640]{1,0:T(8,128)}, f32[16,640]{1,0:T(8,128)}) custom-call(f32[32,16,128]{2,1,0:T(8,128)S(1)} %all_to_all.5.parts, f32[5,16,640]{2,1,0:T(8,128)S(1)} %get-tuple-element.13.sides, f32[6,384,128]{2,1,0:T(8,128)S(1)} %get-tuple-element.20.basis_ext, f32[4,24,768]{2,1,0:T(8,128)S(1)} %get-tuple-element.21.side_ext), custom_call_target="tpu_custom_call" | custom-call | tf_op jit(solution)/shard_map/finish/pallas_call | solution.py:309
  (2 shorter events, 0.0 us)
Async XLA Ops:
  2.0 6.7 %collective-permute-start.2 = (f32[16,128]{1,0:T(8,128)S(1)}, f32[16,128]{1,0:T(8,128)S(1)}, u32[]{:S(2)}, u32[]{:S(2)}) collective-permute-start(f32[16,128]{1,0:T(8,128)S(1)} %get-tuple-element.17), channel_id=1, source_target_pairs={{0,3},{1,0},{2,1},{3,2},{4,7},{5,4},{6,5},{7,6},{8,11},{9,8},{10,9... | collective-permute-start | bytes 24584 | tf_op jit(solution)/shard_map/ppermute | solution.py:344
  7.2 5.4 %collective-permute-start.3 = (f32[16,128]{1,0:T(8,128)S(1)}, f32[16,128]{1,0:T(8,128)S(1)}, u32[]{:S(2)}, u32[]{:S(2)}) collective-permute-start(f32[16,128]{1,0:T(8,128)S(1)} %get-tuple-element.18), channel_id=1, source_target_pairs={{0,1},{1,2},{2,3},{3,0},{4,5},{5,6},{6,7},{7,4},{8,9},{9,10},{10,1... | collective-permute-start | bytes 24584 | tf_op jit(solution)/shard_map/ppermute | solution.py:343
  7.2 9.5 %collective-permute-start = (f32[88,640]{1,0:T(8,128)S(1)}, f32[88,640]{1,0:T(8,128)S(1)}, u32[]{:S(2)}, u32[]{:S(2)}) collective-permute-start(f32[88,640]{1,0:T(8,128)S(1)} %get-tuple-element.15), channel_id=1, source_target_pairs={{0,28},{4,0},{8,4},{12,8},{16,12},{20,16},{24,20},{28,24},{1,29},{... | collective-permute-start | bytes 675848 | tf_op jit(solution)/shard_map/ppermute | solution.py:346
  8.8 7.9 %collective-permute-start.1 = (f32[88,640]{1,0:T(8,128)S(1)}, f32[88,640]{1,0:T(8,128)S(1)}, u32[]{:S(2)}, u32[]{:S(2)}) collective-permute-start(f32[88,640]{1,0:T(8,128)S(1)} %get-tuple-element.16), channel_id=1, source_target_pairs={{0,4},{4,8},{8,12},{12,16},{16,20},{20,24},{24,28},{28,0},{1,5},{5... | collective-permute-start | bytes 675848 | tf_op jit(solution)/shard_map/ppermute | solution.py:345
  12.6 4.1 %collective-permute-start.5 = (f32[32,128]{1,0:T(8,128)S(1)}, f32[32,128]{1,0:T(8,128)S(1)}, u32[]{:S(2)}, u32[]{:S(2)}) collective-permute-start(f32[32,128]{1,0:T(8,128)S(1)} %constant_dynamic-update-slice_fusion), channel_id=1, source_target_pairs={{0,4},{4,8},{8,12},{12,16},{16,20},{20,24},{24,28},{28,0},{1,5},{5... | collective-permute-start | bytes 49160 | tf_op jit(solution)/shard_map/ppermute | solution.py:348
  12.6 4.1 %collective-permute-start.4 = (f32[32,128]{1,0:T(8,128)S(1)}, f32[32,128]{1,0:T(8,128)S(1)}, u32[]{:S(2)}, u32[]{:S(2)}) collective-permute-start(f32[32,128]{1,0:T(8,128)S(1)} %constant_dynamic-update-slice_fusion), channel_id=1, source_target_pairs={{0,28},{4,0},{8,4},{12,8},{16,12},{20,16},{24,20},{28,24},{1,29},{... | collective-permute-start | bytes 49160 | tf_op jit(solution)/shard_map/ppermute | solution.py:349

commit v4 on v3

--- a/solution.py
+++ b/solution.py
@@ -1,5 +1,3 @@
-import functools
-
 import jax
 import jax.numpy as jnp
 from jax import lax
@@ -11,6 +9,7 @@
 ITERS = 3
 DEPTH = ITERS + 1
 LANES = 128
+UNROLL = (11, 10, 9, 8)
 
 
 def ring(count, step):
@@ -56,10 +55,11 @@
     return pltpu.roll(v, by % v.shape[0], 0)
 
 
-def apply_faces(v, diag, k_east, k_north):
-    flux_e = k_east * (v - roll_lanes(v, -1))
-    flux_n = k_north * (v - roll_rows(v, -1))
-    return diag * v + (flux_e - roll_lanes(flux_e, 1)) + (flux_n - roll_rows(flux_n, 1))
+def apply_faces(v, faces, shift=0.0):
+    centre, k_east, k_west, k_north, k_south = faces
+    beside = k_east * roll_lanes(v, -1) + k_west * roll_lanes(v, 1)
+    above = k_north * roll_rows(v, -1) + k_south * roll_rows(v, 1)
+    return (centre - shift) * v - (beside + above)
 
 
 def moments_kernel(
@@ -104,19 +104,20 @@
     wet = jnp.where(beyond_n | beyond_s, 0.0, fields_ext[2])
     k_east = fields_ext[3] * wet * roll_lanes(wet, -1)
     k_north = fields_ext[4] * wet * roll_rows(wet, -1)
-    diag = fields_ext[5] * wet + (1.0 - wet)
-    side_ext[0] = diag
-    side_ext[1] = k_east
-    side_ext[2] = k_north
-    start = fields_ext[1] - apply_faces(fields_ext[0], diag, k_east, k_north)
-    side_ext[3] = start
+    k_west = roll_lanes(k_east, 1)
+    k_south = roll_rows(k_north, 1)
+    centre = fields_ext[5] * wet + k_east + k_west + k_north + k_south + (1.0 - wet)
+    for c, values in enumerate((centre, k_east, k_west, k_north, k_south)):
+        side_ext[c] = values
+    start = fields_ext[1] - apply_faces(fields_ext[0], [side_ext[c] for c in range(5)])
+    side_ext[5] = start
     v = start
     for power in range(ITERS + 1):
         for tile in range(tiles):
             part = v[:rows, tile * LANES : (tile + 1) * LANES]
             start_powers[tile, pl.ds(power * rows, rows), :] = part
         if power < ITERS:
-            v = apply_faces(v, side_ext[0] - SHIFT, side_ext[1], side_ext[2])
+            v = apply_faces(v, [side_ext[c] for c in range(5)], SHIFT)
     spare = (8 - (ITERS + 1)) * rows
     start_powers[:, pl.ds((ITERS + 1) * rows, spare), :] = jnp.zeros(
         (tiles, spare, LANES), jnp.float32
@@ -124,11 +125,11 @@
 
     for q in range(tall):
         ring_row = (q - DEPTH) % tall
-        for c, coeff in enumerate((side_ext.at[0], side_ext.at[1], side_ext.at[2])):
-            spread = jnp.broadcast_to(coeff[ring_row : ring_row + 1, :], (8, wide))
+        for c in range(4):
+            spread = jnp.broadcast_to(side_ext[c, ring_row : ring_row + 1, :], (8, wide))
             faces[c, q] = spread
             if c == 0:
-                faces[3, q] = spread - SHIFT
+                faces[4, q] = spread - SHIFT
         for tile in range(tiles + 1):
             part = basis_ext[tile, pl.ds(ring_row, vectors, stride=tall), :]
             powers[q, :vectors, tile * LANES : (tile + 1) * LANES] = part
@@ -136,27 +137,24 @@
     def coefficient(c, q):
         return jnp.concatenate([faces[c, q]] * (vectors // 8), axis=0)
 
-    unroll = 2
     for power in range(DEPTH):
         first, last = 1 + power, tall - 1 - power
         source = slice(power * vectors, (power + 1) * vectors)
         target = slice((power + 1) * vectors, (power + 2) * vectors)
-        middle = 0 if power == 0 else 3
-
-        def some_rows(i, flux_s, first=first, source=source, target=target, middle=middle):
+        middle = 0 if power == 0 else 4
+        unroll = UNROLL[power]
+
+        def some_rows(i, carry, source=source, target=target, middle=middle, first=first, unroll=unroll):
             for u in range(unroll):
                 q = first + i * unroll + u
                 v = powers[q, source, :]
-                flux_n = coefficient(2, q) * (v - powers[q + 1, source, :])
-                flux_e = coefficient(1, q) * (v - roll_lanes(v, -1))
-                image = coefficient(middle, q) * v + (flux_e - roll_lanes(flux_e, 1))
-                powers[q, target, :] = image + (flux_n - flux_s)
-                flux_s = flux_n
-            return flux_s
-
-        below = first - 1
-        flux = powers[below, source, :] - powers[first, source, :]
-        lax.fori_loop(0, (last - first) // unroll, some_rows, coefficient(2, below) * flux)
+                beside = coefficient(1, q) * roll_lanes(v, -1) + coefficient(2, q) * roll_lanes(v, 1)
+                above = coefficient(3, q) * powers[q + 1, source, :]
+                above += coefficient(3, q - 1) * powers[q - 1, source, :]
+                powers[q, target, :] = coefficient(middle, q) * v - (beside + above)
+            return carry
+
+        lax.fori_loop(0, (last - first) // unroll, some_rows, 0)
 
     base = (ITERS + 2) * vectors
     count = base + 8
@@ -292,14 +290,13 @@
         for i in range(ITERS + 1):
             along[i].append(acc[i])
     along = [jnp.concatenate(pieces, axis=1) for pieces in along]
-    diag, k_east, k_north = side_ext[0], side_ext[1], side_ext[2]
-    image = functools.partial(apply_faces, k_east=k_east, k_north=k_north)
-    v = side_ext[3] + image(along[0], diag)
+    faces = [side_ext[c] for c in range(5)]
+    v = side_ext[5] + apply_faces(along[0], faces)
     x = sides[0] - along[0][:rows, :cols]
     r = rho[0] * v[:rows, :cols]
     for i in range(ITERS):
         x = x + delta[i] * (v + along[i + 1])[:rows, :cols]
-        v = image(v, diag - SHIFT) + image(along[i + 1], diag)
+        v = apply_faces(v, faces, SHIFT) + apply_faces(along[i + 1], faces)
         r = r + rho[i + 1] * v[:rows, :cols]
     solution[...] = x
     residual[...] = r
@@ -350,13 +347,13 @@
     place = jnp.stack([lax.axis_index("lat"), jnp.int32(n_lat)])
     copies, basis_ext, side_ext = call(
         moments_kernel,
-        [f32(devices, vectors, LANES), f32(tiles + 1, vectors * tall, LANES), f32(4, tall, wide)],
+        [f32(devices, vectors, LANES), f32(tiles + 1, vectors * tall, LANES), f32(6, tall, wide)],
         [pltpu.SMEM] + [pltpu.VMEM] * 9,
         (place, basis, sides, mask, from_n, from_s, from_e, from_w, corner_n, corner_s),
         scratch=[
             pltpu.VMEM((tall, (ITERS + 2) * vectors, wide), jnp.float32),
             pltpu.VMEM((6, tall, wide), jnp.float32),
-            pltpu.VMEM((4, tall, 8, wide), jnp.float32),
+            pltpu.VMEM((5, tall, 8, wide), jnp.float32),
             pltpu.VMEM((tiles, 8 * rows, LANES), jnp.float32),
         ],
         name="moments",

time: 44 us -> 40.2 us (0.914)
  Pallas kernels: 14.4 us -> 10.6 us
    pallas_call x3, Pallas kernels: 14.4 us -> 10.6 us  [call(): pl.pallas_call(kernel, out_shape=out_shape, in_specs=[pl.BlockSpec(memory...]
where the time goes in v4:
time: 40.2 us; the launch traced here: 40.1 us
  blocking collectives  14.1 us (35%)
  Pallas kernels  10.6 us (26%)
  starting transfers between devices  9.39 us (23%)
  waiting for transfers between devices  5.2 us (13%)
  between operations  0.66 us (2%)
    all_to_all x1, blocking collectives, shards(): parts = lax.all_to_all(copies, ('lat', 'lon'), 0, 0)  14.1 us
    pallas_call x3, Pallas kernels, call(): pl.pallas_call(kernel, out_shape=out_shape, in_specs=[pl.BlockSpec(memory...  10.6 us
    ppermute x1, starting transfers between devices, shards(): from_e = lax.ppermute(to_w, 'lon', ring(n_lon, -1))  5.13 us
    ppermute x1, waiting for transfers between devices, shards(): from_w = lax.ppermute(to_e, 'lon', ring(n_lon, 1))  3.83 us
    ppermute x1, starting transfers between devices, shards(): corner_n = lax.ppermute(strips, 'lat', south)  2.64 us
    ppermute x1, starting transfers between devices, shards(): from_n = lax.ppermute(to_s, 'lat', south)  1.61 us
    ppermute x1, waiting for transfers between devices, shards(): corner_s = lax.ppermute(strips, 'lat', north)  1.34 us
  transfers between devices with their start and end apart: 6, of which 2 were waited for; matrix products, arithmetic and copies ran while one was open for 0% of the time, Pallas kernels for 0%

profile of v4, /device:TPU:0, one launch (start us, length us, event | category | flops | bytes accessed | tf_op | source)
XLA Modules:
  0.0 40.1 jit_solution(18064934758461738632)
XLA Ops:
  0.6 1.4 %pack.1 = (f32[16,16,640]{2,1,0:T(8,128)S(1)}, f32[5,16,640]{2,1,0:T(8,128)S(1)}, s32[16,640]{1,0:T(8,128)S(1)}, f32[88,640]{1,0:T(8,128)S(1)}, f32[88,640]{1,0:...) custom-call(f32[16,16,640]{2,1,0:T(8,128)} %basis_hbm.1, f32[16,640]{1,0:T(8,128)} %guess_hbm.1, ...), custom_call_target="tpu_custom_call" | custom-call | tf_op jit(solution)/shard_map/pack/pallas_call | solution.py:306
  2.0 5.1 %collective-permute-start.2 = (f32[16,128]{1,0:T(8,128)S(1)}, f32[16,128]{1,0:T(8,128)S(1)}, u32[]{:S(2)}, u32[]{:S(2)}) collective-permute-start(f32[16,128]{1,0:T(8,128)S(1)} %get-tuple-element.17), channel_id=1, source_target_pairs={{0,3},{1,0},{2,1},{3,2},{4,7},{5,4},{6,5},{7,6},{8,11},{9,8},{10,9... | collective-permute-start | bytes 24584 | tf_op jit(solution)/shard_map/ppermute | solution.py:341
  7.2 0.0 collective-permute-start.3
  7.2 1.6 %collective-permute-start = (f32[88,640]{1,0:T(8,128)S(1)}, f32[88,640]{1,0:T(8,128)S(1)}, u32[]{:S(2)}, u32[]{:S(2)}) collective-permute-start(f32[88,640]{1,0:T(8,128)S(1)} %get-tuple-element.15), channel_id=1, source_target_pairs={{0,28},{4,0},{8,4},{12,8},{16,12},{20,16},{24,20},{28,24},{1,29},{... | collective-permute-start | bytes 675848 | tf_op jit(solution)/shard_map/ppermute | solution.py:343
  8.8 0.0 collective-permute-start.1
  8.8 0.0 collective-permute-done.2.from_e
  8.8 3.8 %collective-permute-done.3.from_w = f32[16,128]{1,0:T(8,128)S(1)} collective-permute-done((f32[16,128]{1,0:T(8,128)S(1)}, f32[16,128]{1,0:T(8,128)S(1)}, u32[]{:S(2)}, u32[]{:S(2)}) %collective-permute-start.3) | collective-permute-done | bytes 8224 | tf_op jit(solution)/shard_map/ppermute | solution.py:340
  12.6 0.0 collective-permute-start.5
  12.6 2.6 %collective-permute-start.4 = (f32[32,128]{1,0:T(8,128)S(1)}, f32[32,128]{1,0:T(8,128)S(1)}, u32[]{:S(2)}, u32[]{:S(2)}) collective-permute-start(f32[32,128]{1,0:T(8,128)S(1)} %constant_dynamic-update-slice_fusion), channel_id=1, source_target_pairs={{0,28},{4,0},{8,4},{12,8},{16,12},{20,16},{24,20},{28,24},{1,29},{... | collective-permute-start | bytes 49160 | tf_op jit(solution)/shard_map/ppermute | solution.py:346
  15.3 0.1 pad_add_fusion.place
  15.3 1.3 %collective-permute-done.5.corner_s = f32[32,128]{1,0:T(8,128)S(1)} collective-permute-done((f32[32,128]{1,0:T(8,128)S(1)}, f32[32,128]{1,0:T(8,128)S(1)}, u32[]{:S(2)}, u32[]{:S(2)}) %collective-permute-start.5) | collective-permute-done | bytes 16416 | tf_op jit(solution)/shard_map/ppermute | solution.py:345
  16.7 0.0 collective-permute-done.4.corner_n
  16.7 0.0 collective-permute-done.from_n
  16.7 0.0 collective-permute-done.1.from_s
  16.7 6.0 %moments.1 = (f32[32,16,128]{2,1,0:T(8,128)S(1)}, f32[6,384,128]{2,1,0:T(8,128)S(1)}, f32[6,24,768]{2,1,0:T(8,128)S(1)}) custom-call(s32[2]{0:T(128)S(1)} %pad_add_fusion.place, f32[16,16,640]{2,1,0:T(8,128)S(1)} %get-tuple-element.12.basis, f32[5,16,640]{2,1,0:T(8,128)S(1)} %get-tuple-element.13.sides, s32[16,640]{1,0:T(8,128)S(1)} %get-tuple-element.14.mask, ...), custom_call_target="tpu_custom_call" | custom-call | tf_op jit(solution)/shard_map/moments/pallas_call | solution.py:306
  22.7 14.1 %all_to_all.5.parts = f32[32,16,128]{2,1,0:T(8,128)S(1)} all-to-all(f32[32,16,128]{2,1,0:T(8,128)S(1)} %get-tuple-element.19), channel_id=1, replica_groups=mesh['lat'=8,'lon'=4] {'lat','lon'}, dimensions={0} | all-to-all | bytes 524288 | tf_op jit(solution)/shard_map/all_to_all | solution.py:361
  36.9 3.2 %finish.1 = (f32[16,640]{1,0:T(8,128)}, f32[16,640]{1,0:T(8,128)}) custom-call(f32[32,16,128]{2,1,0:T(8,128)S(1)} %all_to_all.5.parts, f32[5,16,640]{2,1,0:T(8,128)S(1)} %get-tuple-element.13.sides, f32[6,384,128]{2,1,0:T(8,128)S(1)} %get-tuple-element.20.basis_ext, f32[6,24,768]{2,1,0:T(8,128)S(1)} %get-tuple-element.21.side_ext), custom_call_target="tpu_custom_call" | custom-call | tf_op jit(solution)/shard_map/finish/pallas_call | solution.py:306
  (2 shorter events, 0.0 us)
Async XLA Ops:
  2.0 6.7 %collective-permute-start.2 = (f32[16,128]{1,0:T(8,128)S(1)}, f32[16,128]{1,0:T(8,128)S(1)}, u32[]{:S(2)}, u32[]{:S(2)}) collective-permute-start(f32[16,128]{1,0:T(8,128)S(1)} %get-tuple-element.17), channel_id=1, source_target_pairs={{0,3},{1,0},{2,1},{3,2},{4,7},{5,4},{6,5},{7,6},{8,11},{9,8},{10,9... | collective-permute-start | bytes 24584 | tf_op jit(solution)/shard_map/ppermute | solution.py:341
  7.2 5.4 %collective-permute-start.3 = (f32[16,128]{1,0:T(8,128)S(1)}, f32[16,128]{1,0:T(8,128)S(1)}, u32[]{:S(2)}, u32[]{:S(2)}) collective-permute-start(f32[16,128]{1,0:T(8,128)S(1)} %get-tuple-element.18), channel_id=1, source_target_pairs={{0,1},{1,2},{2,3},{3,0},{4,5},{5,6},{6,7},{7,4},{8,9},{9,10},{10,1... | collective-permute-start | bytes 24584 | tf_op jit(solution)/shard_map/ppermute | solution.py:340
  7.2 9.5 %collective-permute-start = (f32[88,640]{1,0:T(8,128)S(1)}, f32[88,640]{1,0:T(8,128)S(1)}, u32[]{:S(2)}, u32[]{:S(2)}) collective-permute-start(f32[88,640]{1,0:T(8,128)S(1)} %get-tuple-element.15), channel_id=1, source_target_pairs={{0,28},{4,0},{8,4},{12,8},{16,12},{20,16},{24,20},{28,24},{1,29},{... | collective-permute-start | bytes 675848 | tf_op jit(solution)/shard_map/ppermute | solution.py:343
  8.8 7.9 %collective-permute-start.1 = (f32[88,640]{1,0:T(8,128)S(1)}, f32[88,640]{1,0:T(8,128)S(1)}, u32[]{:S(2)}, u32[]{:S(2)}) collective-permute-start(f32[88,640]{1,0:T(8,128)S(1)} %get-tuple-element.16), channel_id=1, source_target_pairs={{0,4},{4,8},{8,12},{12,16},{16,20},{20,24},{24,28},{28,0},{1,5},{5... | collective-permute-start | bytes 675848 | tf_op jit(solution)/shard_map/ppermute | solution.py:342
  12.6 4.1 %collective-permute-start.5 = (f32[32,128]{1,0:T(8,128)S(1)}, f32[32,128]{1,0:T(8,128)S(1)}, u32[]{:S(2)}, u32[]{:S(2)}) collective-permute-start(f32[32,128]{1,0:T(8,128)S(1)} %constant_dynamic-update-slice_fusion), channel_id=1, source_target_pairs={{0,4},{4,8},{8,12},{12,16},{16,20},{20,24},{24,28},{28,0},{1,5},{5... | collective-permute-start | bytes 49160 | tf_op jit(solution)/shard_map/ppermute | solution.py:345
  12.6 4.1 %collective-permute-start.4 = (f32[32,128]{1,0:T(8,128)S(1)}, f32[32,128]{1,0:T(8,128)S(1)}, u32[]{:S(2)}, u32[]{:S(2)}) collective-permute-start(f32[32,128]{1,0:T(8,128)S(1)} %constant_dynamic-update-slice_fusion), channel_id=1, source_target_pairs={{0,28},{4,0},{8,4},{12,8},{16,12},{20,16},{24,20},{28,24},{1,29},{... | collective-permute-start | bytes 49160 | tf_op jit(solution)/shard_map/ppermute | solution.py:346

commit v5 on v4

--- a/solution.py
+++ b/solution.py
@@ -9,7 +9,6 @@
 ITERS = 3
 DEPTH = ITERS + 1
 LANES = 128
-UNROLL = (11, 10, 9, 8)
 
 
 def ring(count, step):
@@ -62,122 +61,183 @@
     return (centre - shift) * v - (beside + above)
 
 
-def moments_kernel(
-    place, basis, sides, mask,
-    from_n, from_s, from_e, from_w, corner_n, corner_s,
-    copies, basis_ext, side_ext, powers, fields_ext, faces, start_powers,
+def edges(f, strip_e, strip_w):
+    at = DEPTH * f
+    lane = lax.broadcasted_iota(jnp.int32, strip_e.shape, 1)
+    edge_e = pltpu.roll(strip_e, (-at) % LANES, 1)
+    edge_w = pltpu.roll(strip_w, (LANES - DEPTH - at) % LANES, 1)
+    return jnp.where(lane < DEPTH, edge_e, jnp.where(lane >= LANES - DEPTH, edge_w, 0.0))
+
+
+def faces_of(wet, east, north, surf):
+    k_east = east * wet * roll_lanes(wet, -1)
+    k_north = north * wet * roll_rows(wet, -1)
+    k_west = roll_lanes(k_east, 1)
+    k_south = roll_rows(k_north, 1)
+    centre = surf * wet + k_east + k_west + k_north + k_south + (1.0 - wet)
+    return centre, k_east, k_west, k_north, k_south
+
+
+def spread_faces(side, faces, q, row):
+    for c in range(4):
+        line = side[c, row : row + 1, :]
+        spread = jnp.broadcast_to(line, (8, line.shape[1]))
+        faces[c, q] = spread
+        if c == 0:
+            faces[4, q] = spread - SHIFT
+
+
+def power_rows(powers, faces, power, q, vectors):
+    source = slice(power * vectors, (power + 1) * vectors)
+    target = slice((power + 1) * vectors, (power + 2) * vectors)
+
+    def coefficient(c, q):
+        return jnp.concatenate([faces[c, q]] * (vectors // 8), axis=0)
+
+    v = powers[q, source, :]
+    beside = coefficient(1, q) * roll_lanes(v, -1) + coefficient(2, q) * roll_lanes(v, 1)
+    above = coefficient(3, q) * powers[q + 1, source, :]
+    above += coefficient(3, q - 1) * powers[q - 1, source, :]
+    middle = coefficient(0 if power == 0 else 4, q)
+    powers[q, target, :] = middle * v - (beside + above)
+
+
+def keep_start_powers(v, faces, rows, start_powers):
+    tiles = start_powers.shape[0]
+    for power in range(ITERS + 1):
+        for tile in range(tiles):
+            part = v[:rows, tile * LANES : (tile + 1) * LANES]
+            start_powers[tile, pl.ds(power * rows, rows), :] = part
+        if power < ITERS:
+            v = apply_faces(v, faces, SHIFT)
+    spare = (8 - (ITERS + 1)) * rows
+    start_powers[:, pl.ds((ITERS + 1) * rows, spare), :] = jnp.zeros(
+        (tiles, spare, LANES), jnp.float32
+    )
+
+
+def products(powers, start_powers, batches, rows):
+    tiles = start_powers.shape[0]
+    nt = (((1,), (1,)), ((), ()))
+    high_sum = 0.0
+    cross_sum = 0.0
+    for batch in batches:
+        x = []
+        for r in batch:
+            tail = [start_powers[t, pl.ds(r, 8, stride=rows), :] for t in range(tiles)]
+            tail = jnp.concatenate(tail, axis=1)
+            x.append(jnp.concatenate([powers[r + DEPTH, :, : tiles * LANES], tail], axis=0))
+        x = jnp.concatenate(x, axis=1)
+        high = x.astype(jnp.bfloat16)
+        low = (x - high.astype(jnp.float32)).astype(jnp.bfloat16)
+        high_sum += lax.dot_general(high, high, nt, preferred_element_type=jnp.float32)
+        cross_sum += lax.dot_general(high, low, nt, preferred_element_type=jnp.float32)
+    return high_sum, cross_sum
+
+
+def inner_kernel(
+    basis, sides, mask, from_e, from_w,
+    powers, basis_ext, sums, side, faces, start_powers,
 ):
     vectors, rows, cols = basis.shape
+    tall = rows + 2 * DEPTH
+    tiles = cols // LANES
+    strip_e, strip_w = from_e[...], from_w[...]
+    for k in range(vectors):
+        for tile in range(tiles):
+            basis_ext[tile, pl.ds(tall * k, rows), :] = basis[k, :, tile * LANES : (tile + 1) * LANES]
+        basis_ext[tiles, pl.ds(tall * k, rows), :] = edges(k, strip_e, strip_w)
+    own = (sides[0], sides[1], mask[...].astype(jnp.float32), sides[2], sides[3], sides[4])
+    guess, rhs, wet, east, north, surf = [
+        jnp.concatenate([v, edges(vectors + f, strip_e, strip_w)], axis=1)
+        for f, v in enumerate(own)
+    ]
+    for c, values in enumerate(faces_of(wet, east, north, surf)):
+        side[c] = values
+    for row in range(rows):
+        spread_faces(side, faces, row + DEPTH, row)
+        for tile in range(tiles + 1):
+            part = basis_ext[tile, pl.ds(row, vectors, stride=tall), :]
+            powers[row + DEPTH, :vectors, tile * LANES : (tile + 1) * LANES] = part
+    whole = [side[c] for c in range(5)]
+    keep_start_powers(rhs - apply_faces(guess, whole), whole, rows, start_powers)
+    for power in range(DEPTH):
+        first, last = DEPTH + 1 + power, DEPTH + rows - 1 - power
+        unroll = (last - first) // (2 if power < 2 else 1)
+
+        def some_rows(i, carry, power=power, first=first, unroll=unroll):
+            for u in range(unroll):
+                power_rows(powers, faces, power, first + i * unroll + u, vectors)
+            return carry
+
+        lax.fori_loop(0, (last - first) // unroll, some_rows, 0)
+    middle = range(DEPTH, rows - DEPTH)
+    batches = [middle[at : at + DEPTH] for at in range(0, len(middle), DEPTH)]
+    high_sum, cross_sum = products(powers, start_powers, batches, rows)
+    sums[0] = high_sum
+    sums[1] = cross_sum
+
+
+def outer_kernel(
+    place, basis_in, powers_in, sums, sides, mask,
+    from_n, from_s, from_e, from_w, corner_n, corner_s,
+    copies, basis_ext, powers, side_ext, fields_ext, faces, start_powers,
+):
+    del basis_in, powers_in
+    rows, cols = mask.shape
     wide = cols + LANES
     tall = rows + 2 * DEPTH
     tiles = cols // LANES
-    lane = lax.broadcasted_iota(jnp.int32, (tall, LANES), 1)
-    strip_e = [from_e[...], corner_n[:DEPTH, :], corner_s[rows - DEPTH : rows, :]]
-    strip_w = [from_w[...], corner_n[rows : rows + DEPTH, :], corner_s[2 * rows - DEPTH :, :]]
-    strip_e = jnp.concatenate(strip_e, axis=0)
-    strip_w = jnp.concatenate(strip_w, axis=0)
-
-    def edge_of(f):
-        at = DEPTH * f
-        edge_e = pltpu.roll(strip_e, (-at) % LANES, 1)
-        edge_w = pltpu.roll(strip_w, (LANES - DEPTH - at) % LANES, 1)
-        return jnp.where(lane < DEPTH, edge_e, jnp.where(lane >= LANES - DEPTH, edge_w, 0.0))
+    vectors = basis_ext.shape[1] // tall
+    halo_e = jnp.concatenate([corner_n[:DEPTH, :], corner_s[rows - DEPTH : rows, :]], axis=0)
+    halo_w = [corner_n[rows : rows + DEPTH, :], corner_s[2 * rows - DEPTH :, :]]
+    halo_w = jnp.concatenate(halo_w, axis=0)
+    strip_e = jnp.concatenate([from_e[...], halo_e], axis=0)
+    strip_w = jnp.concatenate([from_w[...], halo_w], axis=0)
 
     for k in range(vectors):
-        at, to = DEPTH * k, tall * k
+        at, to = DEPTH * k, tall * k + rows
         for tile in range(tiles):
             part = pl.ds(tile * LANES, LANES)
-            basis_ext[tile, pl.ds(to, rows), :] = basis[k, :, part]
-            basis_ext[tile, pl.ds(to + rows, DEPTH), :] = from_n[pl.ds(at, DEPTH), part]
-            basis_ext[tile, pl.ds(to + rows + DEPTH, DEPTH), :] = from_s[pl.ds(at, DEPTH), part]
-        basis_ext[tiles, pl.ds(to, tall), :] = edge_of(k)
+            both = [from_n[pl.ds(at, DEPTH), part], from_s[pl.ds(at, DEPTH), part]]
+            basis_ext[tile, pl.ds(to, 2 * DEPTH), :] = jnp.concatenate(both, axis=0)
+        basis_ext[tiles, pl.ds(to, 2 * DEPTH), :] = edges(k, halo_e, halo_w)
     own = (sides.at[0], sides.at[1], mask, sides.at[2], sides.at[3], sides.at[4])
     for f, ref in enumerate(own):
         at = DEPTH * (vectors + f)
         fields_ext[f, :rows, :cols] = ref[...].astype(jnp.float32)
         fields_ext[f, rows : rows + DEPTH, :cols] = from_n[pl.ds(at, DEPTH), :]
         fields_ext[f, rows + DEPTH :, :cols] = from_s[pl.ds(at, DEPTH), :]
-        fields_ext[f, :, cols:] = edge_of(vectors + f)
+        fields_ext[f, :, cols:] = edges(vectors + f, strip_e, strip_w)
     row = lax.broadcasted_iota(jnp.int32, (tall, wide), 0)
     beyond_n = (row >= rows) & (row < rows + DEPTH) & (place[0] == place[1] - 1)
     beyond_s = (row >= rows + DEPTH) & (place[0] == 0)
     wet = jnp.where(beyond_n | beyond_s, 0.0, fields_ext[2])
-    k_east = fields_ext[3] * wet * roll_lanes(wet, -1)
-    k_north = fields_ext[4] * wet * roll_rows(wet, -1)
-    k_west = roll_lanes(k_east, 1)
-    k_south = roll_rows(k_north, 1)
-    centre = fields_ext[5] * wet + k_east + k_west + k_north + k_south + (1.0 - wet)
-    for c, values in enumerate((centre, k_east, k_west, k_north, k_south)):
+    for c, values in enumerate(faces_of(wet, fields_ext[3], fields_ext[4], fields_ext[5])):
         side_ext[c] = values
-    start = fields_ext[1] - apply_faces(fields_ext[0], [side_ext[c] for c in range(5)])
-    side_ext[5] = start
-    v = start
-    for power in range(ITERS + 1):
-        for tile in range(tiles):
-            part = v[:rows, tile * LANES : (tile + 1) * LANES]
-            start_powers[tile, pl.ds(power * rows, rows), :] = part
-        if power < ITERS:
-            v = apply_faces(v, [side_ext[c] for c in range(5)], SHIFT)
-    spare = (8 - (ITERS + 1)) * rows
-    start_powers[:, pl.ds((ITERS + 1) * rows, spare), :] = jnp.zeros(
-        (tiles, spare, LANES), jnp.float32
-    )
 
     for q in range(tall):
         ring_row = (q - DEPTH) % tall
-        for c in range(4):
-            spread = jnp.broadcast_to(side_ext[c, ring_row : ring_row + 1, :], (8, wide))
-            faces[c, q] = spread
-            if c == 0:
-                faces[4, q] = spread - SHIFT
-        for tile in range(tiles + 1):
-            part = basis_ext[tile, pl.ds(ring_row, vectors, stride=tall), :]
-            powers[q, :vectors, tile * LANES : (tile + 1) * LANES] = part
-
-    def coefficient(c, q):
-        return jnp.concatenate([faces[c, q]] * (vectors // 8), axis=0)
-
+        if q <= 2 * DEPTH or q >= rows - 2:
+            spread_faces(side_ext, faces, q, ring_row)
+        if ring_row >= rows:
+            for tile in range(tiles + 1):
+                part = basis_ext[tile, pl.ds(ring_row, vectors, stride=tall), :]
+                powers[q, :vectors, tile * LANES : (tile + 1) * LANES] = part
+    whole = [side_ext[c] for c in range(5)]
+    start = fields_ext[1] - apply_faces(fields_ext[0], whole)
+    side_ext[5] = start
+    keep_start_powers(start, whole, rows, start_powers)
     for power in range(DEPTH):
-        first, last = 1 + power, tall - 1 - power
-        source = slice(power * vectors, (power + 1) * vectors)
-        target = slice((power + 1) * vectors, (power + 2) * vectors)
-        middle = 0 if power == 0 else 4
-        unroll = UNROLL[power]
-
-        def some_rows(i, carry, source=source, target=target, middle=middle, first=first, unroll=unroll):
-            for u in range(unroll):
-                q = first + i * unroll + u
-                v = powers[q, source, :]
-                beside = coefficient(1, q) * roll_lanes(v, -1) + coefficient(2, q) * roll_lanes(v, 1)
-                above = coefficient(3, q) * powers[q + 1, source, :]
-                above += coefficient(3, q - 1) * powers[q - 1, source, :]
-                powers[q, target, :] = coefficient(middle, q) * v - (beside + above)
-            return carry
-
-        lax.fori_loop(0, (last - first) // unroll, some_rows, 0)
-
+        for u in range(DEPTH):
+            power_rows(powers, faces, power, 1 + power + u, vectors)
+            power_rows(powers, faces, power, tall - 2 - power - u, vectors)
+    ends = [range(DEPTH), range(rows - DEPTH, rows)]
+    high_sum, cross_sum = products(powers, start_powers, ends, rows)
+    high_sum += sums[0]
+    cross_sum += sums[1]
     base = (ITERS + 2) * vectors
     count = base + 8
-    batch = 4
-    nt = (((1,), (1,)), ((), ()))
-
-    def one_batch(i, carry):
-        high_sum, cross_sum = carry
-        x = []
-        for u in range(batch):
-            r = i * batch + u
-            tail = [start_powers[t, pl.ds(r, 8, stride=rows), :] for t in range(tiles)]
-            tail = jnp.concatenate(tail, axis=1)
-            x.append(jnp.concatenate([powers[r + DEPTH, :, :cols], tail], axis=0))
-        x = jnp.concatenate(x, axis=1)
-        high = x.astype(jnp.bfloat16)
-        low = (x - high.astype(jnp.float32)).astype(jnp.bfloat16)
-        high_sum += lax.dot_general(high, high, nt, preferred_element_type=jnp.float32)
-        cross_sum += lax.dot_general(high, low, nt, preferred_element_type=jnp.float32)
-        return high_sum, cross_sum
-
-    zero = jnp.zeros((count, count), jnp.float32)
-    high_sum, cross_sum = lax.fori_loop(0, rows // batch, one_batch, (zero, zero))
     full = high_sum + cross_sum + cross_sum.T
     full = jnp.concatenate([full, jnp.zeros((count, LANES - count), jnp.float32)], axis=1)
     at = lax.broadcasted_iota(jnp.int32, (vectors, LANES), 1)
@@ -302,7 +362,7 @@
     residual[...] = r
 
 
-def call(kernel, out_shape, spaces, inputs, scratch=(), name=None):
+def call(kernel, out_shape, spaces, inputs, scratch=(), name=None, flops=10**6, aliases={}):
     return pl.pallas_call(
         kernel,
         out_shape=out_shape,
@@ -310,6 +370,8 @@
         out_specs=[pl.BlockSpec(memory_space=pltpu.VMEM)] * len(out_shape),
         scratch_shapes=scratch,
         name=name,
+        input_output_aliases=aliases,
+        cost_estimate=pl.CostEstimate(flops=flops, bytes_accessed=10**6, transcendentals=0),
         compiler_params=pltpu.CompilerParams(vmem_limit_bytes=24 * 1024 * 1024),
     )(*inputs)
 
@@ -345,18 +407,29 @@
     corner_s = lax.ppermute(strips, "lat", north)
     corner_n = lax.ppermute(strips, "lat", south)
     place = jnp.stack([lax.axis_index("lat"), jnp.int32(n_lat)])
-    copies, basis_ext, side_ext = call(
-        moments_kernel,
-        [f32(devices, vectors, LANES), f32(tiles + 1, vectors * tall, LANES), f32(6, tall, wide)],
-        [pltpu.SMEM] + [pltpu.VMEM] * 9,
-        (place, basis, sides, mask, from_n, from_s, from_e, from_w, corner_n, corner_s),
-        scratch=[
-            pltpu.VMEM((tall, (ITERS + 2) * vectors, wide), jnp.float32),
-            pltpu.VMEM((6, tall, wide), jnp.float32),
-            pltpu.VMEM((5, tall, 8, wide), jnp.float32),
-            pltpu.VMEM((tiles, 8 * rows, LANES), jnp.float32),
-        ],
-        name="moments",
+    count = (ITERS + 2) * vectors
+    powers = f32(tall, count, wide)
+    basis_ext = f32(tiles + 1, vectors * tall, LANES)
+    faces = pltpu.VMEM((5, tall, 8, wide), jnp.float32)
+    start_powers = pltpu.VMEM((tiles, 8 * rows, LANES), jnp.float32)
+    powers, basis_ext, sums = call(
+        inner_kernel,
+        [powers, basis_ext, f32(2, count + 8, count + 8)],
+        [pltpu.VMEM] * 5,
+        (basis, sides, mask, from_e, from_w),
+        scratch=[pltpu.VMEM((5, rows, wide), jnp.float32), faces, start_powers],
+        name="inner",
+        flops=10**9,
+    )
+    copies, basis_ext, _, side_ext = call(
+        outer_kernel,
+        [f32(devices, vectors, LANES), basis_ext, powers, f32(6, tall, wide)],
+        [pltpu.SMEM] + [pltpu.VMEM] * 11,
+        (place, basis_ext, powers, sums, sides, mask)
+        + (from_n, from_s, from_e, from_w, corner_n, corner_s),
+        scratch=[pltpu.VMEM((6, tall, wide), jnp.float32), faces, start_powers],
+        name="outer",
+        aliases={1: 1, 2: 2},
     )
     parts = lax.all_to_all(copies, ("lat", "lon"), 0, 0)
     return call(

time: 40.2 us -> 37.1 us (0.923)
  waiting for transfers between devices: 5.2 us -> 3.77 us
  blocking collectives: 14.1 us -> 12.7 us
    all_to_all x1, blocking collectives: 14.1 us -> 12.7 us  [shards(): parts = lax.all_to_all(copies, ('lat', 'lon'), 0, 0)]
    ppermute x1, waiting for transfers between devices: 1.34 us -> 0.01 us  [shards(): corner_s = lax.ppermute(strips, 'lat', north)]
    pallas_call x3 -> x4, Pallas kernels: 10.6 us -> 10.3 us  [call(): pl.pallas_call(kernel, out_shape=out_shape, in_specs=[pl.BlockSpec(memory...]
  transfers between devices with their start and end apart: 6 -> 6, of which waited for: 2 -> 1; matrix products, arithmetic and copies ran while one was open for 0% -> 0% of each run, Pallas kernels for 0% -> 8%
where the time goes in v5:
time: 37.1 us; the launch traced here: 36.9 us
  blocking collectives  12.7 us (34%)
  Pallas kernels  10.3 us (28%)
  starting transfers between devices  9.39 us (25%)
  waiting for transfers between devices  3.77 us (10%)
  between operations  0.69 us (2%)
    all_to_all x1, blocking collectives, shards(): parts = lax.all_to_all(copies, ('lat', 'lon'), 0, 0)  12.7 us
    pallas_call x4, Pallas kernels, call(): pl.pallas_call(kernel, out_shape=out_shape, in_specs=[pl.BlockSpec(memory...  10.3 us
    ppermute x1, starting transfers between devices, shards(): from_e = lax.ppermute(to_w, 'lon', ring(n_lon, -1))  5.13 us
    ppermute x1, waiting for transfers between devices, shards(): from_w = lax.ppermute(to_e, 'lon', ring(n_lon, 1))  3.76 us
    ppermute x1, starting transfers between devices, shards(): corner_n = lax.ppermute(strips, 'lat', south)  2.64 us
    ppermute x1, starting transfers between devices, shards(): from_n = lax.ppermute(to_s, 'lat', south)  1.61 us
  transfers between devices with their start and end apart: 6, of which 1 were waited for; matrix products, arithmetic and copies ran while one was open for 0% of the time, Pallas kernels for 8%

profile of v5, /device:TPU:0, one launch (start us, length us, event | category | flops | bytes accessed | tf_op | source)
XLA Modules:
  0.0 36.9 jit_solution(13060960269142055921)
XLA Ops:
  0.6 1.4 %pack.1 = (f32[16,16,640]{2,1,0:T(8,128)S(1)}, f32[5,16,640]{2,1,0:T(8,128)S(1)}, s32[16,640]{1,0:T(8,128)S(1)}, f32[88,640]{1,0:T(8,128)S(1)}, f32[88,640]{1,0:...) custom-call(f32[16,16,640]{2,1,0:T(8,128)} %basis_hbm.1, f32[16,640]{1,0:T(8,128)} %guess_hbm.1, ...), custom_call_target="tpu_custom_call" | custom-call | flops 1000000 | bytes 1000000 | tf_op jit(solution)/shard_map/pack/pallas_call | solution.py:366
  2.0 5.1 %collective-permute-start = (f32[16,128]{1,0:T(8,128)S(1)}, f32[16,128]{1,0:T(8,128)S(1)}, u32[]{:S(2)}, u32[]{:S(2)}) collective-permute-start(f32[16,128]{1,0:T(8,128)S(1)} %get-tuple-element.18), channel_id=1, source_target_pairs={{0,3},{1,0},{2,1},{3,2},{4,7},{5,4},{6,5},{7,6},{8,11},{9,8},{10,9... | collective-permute-start | bytes 24584 | tf_op jit(solution)/shard_map/ppermute | solution.py:403
  7.2 0.0 collective-permute-start.1
  7.2 1.6 %collective-permute-start.2 = (f32[88,640]{1,0:T(8,128)S(1)}, f32[88,640]{1,0:T(8,128)S(1)}, u32[]{:S(2)}, u32[]{:S(2)}) collective-permute-start(f32[88,640]{1,0:T(8,128)S(1)} %get-tuple-element.23), channel_id=1, source_target_pairs={{0,28},{4,0},{8,4},{12,8},{16,12},{20,16},{24,20},{28,24},{1,29},{... | collective-permute-start | bytes 675848 | tf_op jit(solution)/shard_map/ppermute | solution.py:405
  8.8 0.0 collective-permute-start.3
  8.8 0.1 pad_add_fusion.place
  8.9 0.0 collective-permute-done.from_e
  8.9 3.8 %collective-permute-done.1.from_w = f32[16,128]{1,0:T(8,128)S(1)} collective-permute-done((f32[16,128]{1,0:T(8,128)S(1)}, f32[16,128]{1,0:T(8,128)S(1)}, u32[]{:S(2)}, u32[]{:S(2)}) %collective-permute-start.1) | collective-permute-done | bytes 8224 | tf_op jit(solution)/shard_map/ppermute | solution.py:402
  12.6 0.0 collective-permute-start.5
  12.6 2.6 %collective-permute-start.4 = (f32[32,128]{1,0:T(8,128)S(1)}, f32[32,128]{1,0:T(8,128)S(1)}, u32[]{:S(2)}, u32[]{:S(2)}) collective-permute-start(f32[32,128]{1,0:T(8,128)S(1)} %constant_dynamic-update-slice_fusion), channel_id=1, source_target_pairs={{0,28},{4,0},{8,4},{12,8},{16,12},{20,16},{24,20},{28,24},{1,29},{... | collective-permute-start | bytes 49160 | tf_op jit(solution)/shard_map/ppermute | solution.py:408
  15.3 2.9 %inner.1 = (f32[24,80,768]{2,1,0:T(8,128)S(1)}, f32[6,384,128]{2,1,0:T(8,128)S(1)}, f32[2,88,88]{2,1,0:T(8,128)S(1)}) custom-call(f32[16,16,640]{2,1,0:T(8,128)S(1)} %get-tuple-element.15.basis, f32[5,16,640]{2,1,0:T(8,128)S(1)} %get-tuple-element.16.sides, s32[16,640]{1,0:T(8,128)S(1)} %get-tuple-element.17.mask, ...), custom_call_target="tpu_custom_call" | custom-call | flops 1000000000 | bytes 1000000 | tf_op jit(solution)/shard_map/inner/pallas_call | solution.py:366
  18.1 0.0 collective-permute-done.5.corner_s
  18.2 0.0 collective-permute-done.4.corner_n
  18.2 0.0 collective-permute-done.2.from_n
  18.2 0.0 collective-permute-done.3.from_s
  18.2 2.8 %outer.1 = (f32[32,16,128]{2,1,0:T(8,128)S(1)}, f32[6,384,128]{2,1,0:T(8,128)S(1)}, f32[24,80,768]{2,1,0:T(8,128)S(1)}, f32[6,24,768]{2,1,0:T(8,128)S(1)}) custom-call(s32[2]{0:T(128)S(1)} %pad_add_fusion.place, f32[6,384,128]{2,1,0:T(8,128)S(1)} %get-tuple-element.20.basis_in, ...), custom_call_target="tpu_custom_call", output_to_operand_aliasing={{1}: (1, {}), {2}: (2, {})} | custom-call | flops 1000000 | bytes 1000000 | tf_op jit(solution)/shard_map/outer/pallas_call | solution.py:366
  21.0 12.7 %all_to_all.5.parts = f32[32,16,128]{2,1,0:T(8,128)S(1)} all-to-all(f32[32,16,128]{2,1,0:T(8,128)S(1)} %get-tuple-element.25), channel_id=1, replica_groups=mesh['lat'=8,'lon'=4] {'lat','lon'}, dimensions={0} | all-to-all | bytes 524288 | tf_op jit(solution)/shard_map/all_to_all | solution.py:434
  33.7 3.2 %finish.1 = (f32[16,640]{1,0:T(8,128)}, f32[16,640]{1,0:T(8,128)}) custom-call(f32[32,16,128]{2,1,0:T(8,128)S(1)} %all_to_all.5.parts, f32[5,16,640]{2,1,0:T(8,128)S(1)} %get-tuple-element.16.sides, f32[6,384,128]{2,1,0:T(8,128)S(1)} %get-tuple-element.26.basis_ext, f32[6,24,768]{2,1,0:T(8,128)S(1)} %get-tuple-element.27.side_ext), custom_call_target="tpu_custom_call" | custom-call | flops 1000000 | bytes 1000000 | tf_op jit(solution)/shard_map/finish/pallas_call | solution.py:366
  (2 shorter events, 0.0 us)
Async XLA Ops:
  2.0 6.8 %collective-permute-start = (f32[16,128]{1,0:T(8,128)S(1)}, f32[16,128]{1,0:T(8,128)S(1)}, u32[]{:S(2)}, u32[]{:S(2)}) collective-permute-start(f32[16,128]{1,0:T(8,128)S(1)} %get-tuple-element.18), channel_id=1, source_target_pairs={{0,3},{1,0},{2,1},{3,2},{4,7},{5,4},{6,5},{7,6},{8,11},{9,8},{10,9... | collective-permute-start | bytes 24584 | tf_op jit(solution)/shard_map/ppermute | solution.py:403
  7.2 5.4 %collective-permute-start.1 = (f32[16,128]{1,0:T(8,128)S(1)}, f32[16,128]{1,0:T(8,128)S(1)}, u32[]{:S(2)}, u32[]{:S(2)}) collective-permute-start(f32[16,128]{1,0:T(8,128)S(1)} %get-tuple-element.19), channel_id=1, source_target_pairs={{0,1},{1,2},{2,3},{3,0},{4,5},{5,6},{6,7},{7,4},{8,9},{9,10},{10,1... | collective-permute-start | bytes 24584 | tf_op jit(solution)/shard_map/ppermute | solution.py:402
  7.2 11.0 %collective-permute-start.2 = (f32[88,640]{1,0:T(8,128)S(1)}, f32[88,640]{1,0:T(8,128)S(1)}, u32[]{:S(2)}, u32[]{:S(2)}) collective-permute-start(f32[88,640]{1,0:T(8,128)S(1)} %get-tuple-element.23), channel_id=1, source_target_pairs={{0,28},{4,0},{8,4},{12,8},{16,12},{20,16},{24,20},{28,24},{1,29},{... | collective-permute-start | bytes 675848 | tf_op jit(solution)/shard_map/ppermute | solution.py:405
  8.8 9.4 %collective-permute-start.3 = (f32[88,640]{1,0:T(8,128)S(1)}, f32[88,640]{1,0:T(8,128)S(1)}, u32[]{:S(2)}, u32[]{:S(2)}) collective-permute-start(f32[88,640]{1,0:T(8,128)S(1)} %get-tuple-element.24), channel_id=1, source_target_pairs={{0,4},{4,8},{8,12},{12,16},{16,20},{20,24},{24,28},{28,0},{1,5},{5... | collective-permute-start | bytes 675848 | tf_op jit(solution)/shard_map/ppermute | solution.py:404
  12.6 5.5 %collective-permute-start.5 = (f32[32,128]{1,0:T(8,128)S(1)}, f32[32,128]{1,0:T(8,128)S(1)}, u32[]{:S(2)}, u32[]{:S(2)}) collective-permute-start(f32[32,128]{1,0:T(8,128)S(1)} %constant_dynamic-update-slice_fusion), channel_id=1, source_target_pairs={{0,4},{4,8},{8,12},{12,16},{16,20},{20,24},{24,28},{28,0},{1,5},{5... | collective-permute-start | bytes 49160 | tf_op jit(solution)/shard_map/ppermute | solution.py:407
  12.6 5.5 %collective-permute-start.4 = (f32[32,128]{1,0:T(8,128)S(1)}, f32[32,128]{1,0:T(8,128)S(1)}, u32[]{:S(2)}, u32[]{:S(2)}) collective-permute-start(f32[32,128]{1,0:T(8,128)S(1)} %constant_dynamic-update-slice_fusion), channel_id=1, source_target_pairs={{0,28},{4,0},{8,4},{12,8},{16,12},{20,16},{24,20},{28,24},{1,29},{... | collective-permute-start | bytes 49160 | tf_op jit(solution)/shard_map/ppermute | solution.py:408

commit v6 on v5

--- a/solution.py
+++ b/solution.py
@@ -179,7 +179,7 @@
 
 
 def outer_kernel(
-    place, basis_in, powers_in, sums, sides, mask,
+    inside, basis_in, powers_in, sums, sides, mask,
     from_n, from_s, from_e, from_w, corner_n, corner_s,
     copies, basis_ext, powers, side_ext, fields_ext, faces, start_powers,
 ):
@@ -209,10 +209,8 @@
         fields_ext[f, rows : rows + DEPTH, :cols] = from_n[pl.ds(at, DEPTH), :]
         fields_ext[f, rows + DEPTH :, :cols] = from_s[pl.ds(at, DEPTH), :]
         fields_ext[f, :, cols:] = edges(vectors + f, strip_e, strip_w)
-    row = lax.broadcasted_iota(jnp.int32, (tall, wide), 0)
-    beyond_n = (row >= rows) & (row < rows + DEPTH) & (place[0] == place[1] - 1)
-    beyond_s = (row >= rows + DEPTH) & (place[0] == 0)
-    wet = jnp.where(beyond_n | beyond_s, 0.0, fields_ext[2])
+    wet_halo = fields_ext[2, rows:, :] * jnp.concatenate([inside[...]] * (wide // LANES), axis=1)
+    wet = jnp.concatenate([fields_ext[2, :rows, :], wet_halo], axis=0)
     for c, values in enumerate(faces_of(wet, fields_ext[3], fields_ext[4], fields_ext[5])):
         side_ext[c] = values
 
@@ -362,14 +360,13 @@
     residual[...] = r
 
 
-def call(kernel, out_shape, spaces, inputs, scratch=(), name=None, flops=10**6, aliases={}):
+def call(kernel, out_shape, spaces, inputs, scratch=(), flops=10**6, aliases={}):
     return pl.pallas_call(
         kernel,
         out_shape=out_shape,
         in_specs=[pl.BlockSpec(memory_space=space) for space in spaces],
         out_specs=[pl.BlockSpec(memory_space=pltpu.VMEM)] * len(out_shape),
         scratch_shapes=scratch,
-        name=name,
         input_output_aliases=aliases,
         cost_estimate=pl.CostEstimate(flops=flops, bytes_accessed=10**6, transcendentals=0),
         compiler_params=pltpu.CompilerParams(vmem_limit_bytes=24 * 1024 * 1024),
@@ -396,7 +393,6 @@
         [pltpu.HBM] * 7,
         [pltpu.with_memory_space_constraint(array, pltpu.HBM) for array in own],
         scratch=[pltpu.SemaphoreType.DMA((7,))],
-        name="pack",
     )
     north, south = ring(n_lat, 1), ring(n_lat, -1)
     from_w = lax.ppermute(to_e, "lon", ring(n_lon, 1))
@@ -406,7 +402,9 @@
     strips = jnp.concatenate([from_e, from_w], axis=0)
     corner_s = lax.ppermute(strips, "lat", north)
     corner_n = lax.ppermute(strips, "lat", south)
-    place = jnp.stack([lax.axis_index("lat"), jnp.int32(n_lat)])
+    here = lax.axis_index("lat")
+    inside = jnp.stack([here < n_lat - 1, here > 0]).astype(jnp.float32)
+    inside = jnp.broadcast_to(inside[:, None, None], (2, DEPTH, LANES)).reshape(-1, LANES)
     count = (ITERS + 2) * vectors
     powers = f32(tall, count, wide)
     basis_ext = f32(tiles + 1, vectors * tall, LANES)
@@ -418,17 +416,15 @@
         [pltpu.VMEM] * 5,
         (basis, sides, mask, from_e, from_w),
         scratch=[pltpu.VMEM((5, rows, wide), jnp.float32), faces, start_powers],
-        name="inner",
         flops=10**9,
     )
     copies, basis_ext, _, side_ext = call(
         outer_kernel,
         [f32(devices, vectors, LANES), basis_ext, powers, f32(6, tall, wide)],
-        [pltpu.SMEM] + [pltpu.VMEM] * 11,
-        (place, basis_ext, powers, sums, sides, mask)
+        [pltpu.VMEM] * 12,
+        (inside, basis_ext, powers, sums, sides, mask)
         + (from_n, from_s, from_e, from_w, corner_n, corner_s),
         scratch=[pltpu.VMEM((6, tall, wide), jnp.float32), faces, start_powers],
-        name="outer",
         aliases={1: 1, 2: 2},
     )
     parts = lax.all_to_all(copies, ("lat", "lon"), 0, 0)
@@ -438,7 +434,6 @@
         [pltpu.VMEM] * 4,
         (parts, sides, basis_ext, side_ext),
         scratch=[pltpu.VMEM((ITERS + 1, vectors, LANES), jnp.float32)],
-        name="finish",
     )
 
 

time: 37.1 us -> 36.6 us (0.987)
  Pallas kernels: 10.3 us -> 9.76 us
    pallas_call x4, Pallas kernels: 10.3 us -> 9.76 us  [call(): pl.pallas_call(kernel, out_shape=out_shape, in_specs=[pl.BlockSpec(memory...]
  transfers between devices with their start and end apart: 6 -> 6, of which waited for: 1 -> 1; matrix products, arithmetic and copies ran while one was open for 0% -> 1% of each run, Pallas kernels for 8% -> 8%
where the time goes in v6:
time: 36.6 us; the launch traced here: 36.4 us
  blocking collectives  12.7 us (35%)
  Pallas kernels  9.76 us (27%)
  starting transfers between devices  9.39 us (26%)
  waiting for transfers between devices  3.61 us (10%)
  between operations  0.7 us (2%)
    all_to_all x1, blocking collectives, shards(): parts = lax.all_to_all(copies, ('lat', 'lon'), 0, 0)  12.7 us
    pallas_call x4, Pallas kernels, call(): pl.pallas_call(kernel, out_shape=out_shape, in_specs=[pl.BlockSpec(memory...  9.76 us
    ppermute x1, starting transfers between devices, shards(): from_e = lax.ppermute(to_w, 'lon', ring(n_lon, -1))  5.13 us
    ppermute x1, waiting for transfers between devices, shards(): from_w = lax.ppermute(to_e, 'lon', ring(n_lon, 1))  3.6 us
    ppermute x1, starting transfers between devices, shards(): corner_n = lax.ppermute(strips, 'lat', south)  2.64 us
    ppermute x1, starting transfers between devices, shards(): from_n = lax.ppermute(to_s, 'lat', south)  1.61 us
  transfers between devices with their start and end apart: 6, of which 1 were waited for; matrix products, arithmetic and copies ran while one was open for 1% of the time, Pallas kernels for 8%

profile of v6, /device:TPU:0, one launch (start us, length us, event | category | flops | bytes accessed | tf_op | source)
XLA Modules:
  0.0 36.4 jit_solution(17334897829444851889)
XLA Ops:
  0.6 1.4 %shard_map.86 = (f32[16,16,640]{2,1,0:T(8,128)S(1)}, f32[5,16,640]{2,1,0:T(8,128)S(1)}, s32[16,640]{1,0:T(8,128)S(1)}, f32[88,640]{1,0:T(8,128)S(1)}, f32[88,640...) custom-call(f32[16,16,640]{2,1,0:T(8,128)} %basis_hbm.1, f32[16,640]{1,0:T(8,128)} %guess_hbm.1, ...), custom_call_target="tpu_custom_call" | custom-call | flops 1000000 | bytes 1000000 | tf_op jit(solution)/shard_map/pallas_call | solution.py:364
  2.0 5.1 %collective-permute-start = (f32[16,128]{1,0:T(8,128)S(1)}, f32[16,128]{1,0:T(8,128)S(1)}, u32[]{:S(2)}, u32[]{:S(2)}) collective-permute-start(f32[16,128]{1,0:T(8,128)S(1)} %get-tuple-element.18), channel_id=1, source_target_pairs={{0,3},{1,0},{2,1},{3,2},{4,7},{5,4},{6,5},{7,6},{8,11},{9,8},{10,9... | collective-permute-start | bytes 24584 | tf_op jit(solution)/shard_map/ppermute | solution.py:399
  7.2 0.0 collective-permute-start.1
  7.2 1.6 %collective-permute-start.2 = (f32[88,640]{1,0:T(8,128)S(1)}, f32[88,640]{1,0:T(8,128)S(1)}, u32[]{:S(2)}, u32[]{:S(2)}) collective-permute-start(f32[88,640]{1,0:T(8,128)S(1)} %get-tuple-element.23), channel_id=1, source_target_pairs={{0,28},{4,0},{8,4},{12,8},{16,12},{20,16},{24,20},{28,24},{1,29},{... | collective-permute-start | bytes 675848 | tf_op jit(solution)/shard_map/ppermute | solution.py:401
  8.8 0.0 collective-permute-start.3
  8.8 0.1 add_convert_fusion
  8.9 0.1 broadcast_in_dim.10
  8.9 0.1 broadcast_in_dim.11
  9.0 0.0 collective-permute-done.from_e
  9.0 3.6 %collective-permute-done.1.from_w = f32[16,128]{1,0:T(8,128)S(1)} collective-permute-done((f32[16,128]{1,0:T(8,128)S(1)}, f32[16,128]{1,0:T(8,128)S(1)}, u32[]{:S(2)}, u32[]{:S(2)}) %collective-permute-start.1) | collective-permute-done | bytes 8224 | tf_op jit(solution)/shard_map/ppermute | solution.py:398
  12.6 0.0 collective-permute-start.5
  12.6 2.6 %collective-permute-start.4 = (f32[32,128]{1,0:T(8,128)S(1)}, f32[32,128]{1,0:T(8,128)S(1)}, u32[]{:S(2)}, u32[]{:S(2)}) collective-permute-start(f32[32,128]{1,0:T(8,128)S(1)} %constant_dynamic-update-slice_fusion), channel_id=1, source_target_pairs={{0,28},{4,0},{8,4},{12,8},{16,12},{20,16},{24,20},{28,24},{1,29},{... | collective-permute-start | bytes 49160 | tf_op jit(solution)/shard_map/ppermute | solution.py:404
  15.3 2.9 %shard_map.87 = (f32[24,80,768]{2,1,0:T(8,128)S(1)}, f32[6,384,128]{2,1,0:T(8,128)S(1)}, f32[2,88,88]{2,1,0:T(8,128)S(1)}) custom-call(f32[16,16,640]{2,1,0:T(8,128)S(1)} %get-tuple-element.15.basis, f32[5,16,640]{2,1,0:T(8,128)S(1)} %get-tuple-element.16.sides, s32[16,640]{1,0:T(8,128)S(1)} %get-tuple-element.17.mask, ...), custom_call_target="tpu_custom_call" | custom-call | flops 1000000000 | bytes 1000000 | tf_op jit(solution)/shard_map/pallas_call | solution.py:364
  18.1 0.0 collective-permute-done.5.corner_s
  18.2 0.0 collective-permute-done.4.corner_n
  18.2 0.0 collective-permute-done.2.from_n
  18.2 0.0 collective-permute-done.3.from_s
  18.2 0.1 broadcast_in_dim.12.inside
  18.3 2.3 %shard_map.88 = (f32[32,16,128]{2,1,0:T(8,128)S(1)}, f32[6,384,128]{2,1,0:T(8,128)S(1)}, f32[24,80,768]{2,1,0:T(8,128)S(1)}, f32[6,24,768]{2,1,0:T(8,128)S(1)}) custom-call(f32[8,128]{1,0:T(8,128)S(1)} %broadcast_in_dim.12.inside, f32[6,384,128]{2,1,0:T(8,128)S(1)} %get-tuple-element.20.basis_in, ...), custom_call_target="tpu_custom_call", output_to_operand_aliasing={{1}: (1, {}), {2}: (2, {})} | custom-call | flops 1000000 | bytes 1000000 | tf_op jit(solution)/shard_map/pallas_call | solution.py:364
  20.5 12.7 %all_to_all.5.parts = f32[32,16,128]{2,1,0:T(8,128)S(1)} all-to-all(f32[32,16,128]{2,1,0:T(8,128)S(1)} %get-tuple-element.25), channel_id=1, replica_groups=mesh['lat'=8,'lon'=4] {'lat','lon'}, dimensions={0} | all-to-all | bytes 524288 | tf_op jit(solution)/shard_map/all_to_all | solution.py:430
  33.2 3.2 %shard_map.89 = (f32[16,640]{1,0:T(8,128)}, f32[16,640]{1,0:T(8,128)}) custom-call(f32[32,16,128]{2,1,0:T(8,128)S(1)} %all_to_all.5.parts, f32[5,16,640]{2,1,0:T(8,128)S(1)} %get-tuple-element.16.sides, f32[6,384,128]{2,1,0:T(8,128)S(1)} %get-tuple-element.26.basis_ext, f32[6,24,768]{2,1,0:T(8,128)S(1)} %get-tuple-element.27.side_ext), custom_call_target="tpu_custom_call" | custom-call | flops 1000000 | bytes 1000000 | tf_op jit(solution)/shard_map/pallas_call | solution.py:364
  (2 shorter events, 0.0 us)
Async XLA Ops:
  2.0 7.0 %collective-permute-start = (f32[16,128]{1,0:T(8,128)S(1)}, f32[16,128]{1,0:T(8,128)S(1)}, u32[]{:S(2)}, u32[]{:S(2)}) collective-permute-start(f32[16,128]{1,0:T(8,128)S(1)} %get-tuple-element.18), channel_id=1, source_target_pairs={{0,3},{1,0},{2,1},{3,2},{4,7},{5,4},{6,5},{7,6},{8,11},{9,8},{10,9... | collective-permute-start | bytes 24584 | tf_op jit(solution)/shard_map/ppermute | solution.py:399
  7.2 5.4 %collective-permute-start.1 = (f32[16,128]{1,0:T(8,128)S(1)}, f32[16,128]{1,0:T(8,128)S(1)}, u32[]{:S(2)}, u32[]{:S(2)}) collective-permute-start(f32[16,128]{1,0:T(8,128)S(1)} %get-tuple-element.19), channel_id=1, source_target_pairs={{0,1},{1,2},{2,3},{3,0},{4,5},{5,6},{6,7},{7,4},{8,9},{9,10},{10,1... | collective-permute-start | bytes 24584 | tf_op jit(solution)/shard_map/ppermute | solution.py:398
  7.2 11.0 %collective-permute-start.2 = (f32[88,640]{1,0:T(8,128)S(1)}, f32[88,640]{1,0:T(8,128)S(1)}, u32[]{:S(2)}, u32[]{:S(2)}) collective-permute-start(f32[88,640]{1,0:T(8,128)S(1)} %get-tuple-element.23), channel_id=1, source_target_pairs={{0,28},{4,0},{8,4},{12,8},{16,12},{20,16},{24,20},{28,24},{1,29},{... | collective-permute-start | bytes 675848 | tf_op jit(solution)/shard_map/ppermute | solution.py:401
  8.8 9.4 %collective-permute-start.3 = (f32[88,640]{1,0:T(8,128)S(1)}, f32[88,640]{1,0:T(8,128)S(1)}, u32[]{:S(2)}, u32[]{:S(2)}) collective-permute-start(f32[88,640]{1,0:T(8,128)S(1)} %get-tuple-element.24), channel_id=1, source_target_pairs={{0,4},{4,8},{8,12},{12,16},{16,20},{20,24},{24,28},{28,0},{1,5},{5... | collective-permute-start | bytes 675848 | tf_op jit(solution)/shard_map/ppermute | solution.py:400
  12.6 5.5 %collective-permute-start.5 = (f32[32,128]{1,0:T(8,128)S(1)}, f32[32,128]{1,0:T(8,128)S(1)}, u32[]{:S(2)}, u32[]{:S(2)}) collective-permute-start(f32[32,128]{1,0:T(8,128)S(1)} %constant_dynamic-update-slice_fusion), channel_id=1, source_target_pairs={{0,4},{4,8},{8,12},{12,16},{16,20},{20,24},{24,28},{28,0},{1,5},{5... | collective-permute-start | bytes 49160 | tf_op jit(solution)/shard_map/ppermute | solution.py:403
  12.6 5.5 %collective-permute-start.4 = (f32[32,128]{1,0:T(8,128)S(1)}, f32[32,128]{1,0:T(8,128)S(1)}, u32[]{:S(2)}, u32[]{:S(2)}) collective-permute-start(f32[32,128]{1,0:T(8,128)S(1)} %constant_dynamic-update-slice_fusion), channel_id=1, source_target_pairs={{0,28},{4,0},{8,4},{12,8},{16,12},{20,16},{24,20},{28,24},{1,29},{... | collective-permute-start | bytes 49160 | tf_op jit(solution)/shard_map/ppermute | solution.py:404

commit v7 on v6

--- a/solution.py
+++ b/solution.py
@@ -119,8 +119,7 @@
 def products(powers, start_powers, batches, rows):
     tiles = start_powers.shape[0]
     nt = (((1,), (1,)), ((), ()))
-    high_sum = 0.0
-    cross_sum = 0.0
+    total = 0.0
     for batch in batches:
         x = []
         for r in batch:
@@ -130,9 +129,9 @@
         x = jnp.concatenate(x, axis=1)
         high = x.astype(jnp.bfloat16)
         low = (x - high.astype(jnp.float32)).astype(jnp.bfloat16)
-        high_sum += lax.dot_general(high, high, nt, preferred_element_type=jnp.float32)
-        cross_sum += lax.dot_general(high, low, nt, preferred_element_type=jnp.float32)
-    return high_sum, cross_sum
+        both = jnp.concatenate([high, low], axis=0)
+        total += lax.dot_general(both, high, nt, preferred_element_type=jnp.float32)
+    return total
 
 
 def inner_kernel(
@@ -173,9 +172,7 @@
         lax.fori_loop(0, (last - first) // unroll, some_rows, 0)
     middle = range(DEPTH, rows - DEPTH)
     batches = [middle[at : at + DEPTH] for at in range(0, len(middle), DEPTH)]
-    high_sum, cross_sum = products(powers, start_powers, batches, rows)
-    sums[0] = high_sum
-    sums[1] = cross_sum
+    sums[...] = products(powers, start_powers, batches, rows)
 
 
 def outer_kernel(
@@ -231,12 +228,10 @@
             power_rows(powers, faces, power, 1 + power + u, vectors)
             power_rows(powers, faces, power, tall - 2 - power - u, vectors)
     ends = [range(DEPTH), range(rows - DEPTH, rows)]
-    high_sum, cross_sum = products(powers, start_powers, ends, rows)
-    high_sum += sums[0]
-    cross_sum += sums[1]
+    both = products(powers, start_powers, ends, rows) + sums[...]
     base = (ITERS + 2) * vectors
     count = base + 8
-    full = high_sum + cross_sum + cross_sum.T
+    full = both[:count] + both[count:] + both[count:].T
     full = jnp.concatenate([full, jnp.zeros((count, LANES - count), jnp.float32)], axis=1)
     at = lax.broadcasted_iota(jnp.int32, (vectors, LANES), 1)
     slabs = [full[a * vectors : (a + 1) * vectors, :] for a in range(4)]
@@ -283,10 +278,21 @@
     lane = lax.broadcasted_iota(jnp.int32, (vectors, LANES), 1)
     sub = lax.broadcasted_iota(jnp.int32, (vectors, LANES), 0)
     table = total
+    columns = [jnp.broadcast_to(total[:, i : i + 1], total.shape) for i in range(vectors)]
+
+    def row_of(values, i):
+        return jnp.broadcast_to(values[i : i + 1, :], values.shape)
+
     for i in range(vectors):
-        column = table[:, i : i + 1]
-        pivot_row = table[i : i + 1, :] / table[i : i + 1, i : i + 1]
-        table = jnp.where(sub == i, pivot_row, table - column * pivot_row)
+        column = columns[i]
+        inverse = 1.0 / row_of(column, i)
+
+        def eliminate(values):
+            pivot_row = row_of(values, i) * inverse
+            return jnp.where(sub == i, pivot_row, values - column * pivot_row)
+
+        columns[i + 1 :] = [eliminate(values) for values in columns[i + 1 :]]
+        table = eliminate(table)
     own_lane = (lane % vectors) == sub
     z = [-table[:, free : free + 1]]
     sums = jnp.zeros((vectors, LANES), jnp.float32)
@@ -412,7 +418,7 @@
     start_powers = pltpu.VMEM((tiles, 8 * rows, LANES), jnp.float32)
     powers, basis_ext, sums = call(
         inner_kernel,
-        [powers, basis_ext, f32(2, count + 8, count + 8)],
+        [powers, basis_ext, f32(2 * (count + 8), count + 8)],
         [pltpu.VMEM] * 5,
         (basis, sides, mask, from_e, from_w),
         scratch=[pltpu.VMEM((5, rows, wide), jnp.float32), faces, start_powers],

time: 36.6 us -> 35.5 us (0.970)
  Pallas kernels: 9.76 us -> 8.66 us
    pallas_call x4, Pallas kernels: 9.76 us -> 8.66 us  [call(): pl.pallas_call(kernel, out_shape=out_shape, in_specs=[pl.BlockSpec(memory...]
where the time goes in v7:
time: 35.5 us; the launch traced here: 35.3 us
  blocking collectives  12.7 us (36%)
  starting transfers between devices  9.39 us (26%)
  Pallas kernels  8.66 us (24%)
  waiting for transfers between devices  3.61 us (10%)
  between operations  0.69 us (2%)
    all_to_all x1, blocking collectives, shards(): parts = lax.all_to_all(copies, ('lat', 'lon'), 0, 0)  12.7 us
    pallas_call x4, Pallas kernels, call(): pl.pallas_call(kernel, out_shape=out_shape, in_specs=[pl.BlockSpec(memory...  8.66 us
    ppermute x1, starting transfers between devices, shards(): from_e = lax.ppermute(to_w, 'lon', ring(n_lon, -1))  5.13 us
    ppermute x1, waiting for transfers between devices, shards(): from_w = lax.ppermute(to_e, 'lon', ring(n_lon, 1))  3.6 us
    ppermute x1, starting transfers between devices, shards(): corner_n = lax.ppermute(strips, 'lat', south)  2.64 us
    ppermute x1, starting transfers between devices, shards(): from_n = lax.ppermute(to_s, 'lat', south)  1.61 us
  transfers between devices with their start and end apart: 6, of which 1 were waited for; matrix products, arithmetic and copies ran while one was open for 1% of the time, Pallas kernels for 8%

profile of v7, /device:TPU:0, one launch (start us, length us, event | category | flops | bytes accessed | tf_op | source)
XLA Modules:
  0.0 35.3 jit_solution(2229132284184203008)
XLA Ops:
  0.6 1.4 %shard_map.86 = (f32[16,16,640]{2,1,0:T(8,128)S(1)}, f32[5,16,640]{2,1,0:T(8,128)S(1)}, s32[16,640]{1,0:T(8,128)S(1)}, f32[88,640]{1,0:T(8,128)S(1)}, f32[88,640...) custom-call(f32[16,16,640]{2,1,0:T(8,128)} %basis_hbm.1, f32[16,640]{1,0:T(8,128)} %guess_hbm.1, ...), custom_call_target="tpu_custom_call" | custom-call | flops 1000000 | bytes 1000000 | tf_op jit(solution)/shard_map/pallas_call | solution.py:370
  2.0 5.1 %collective-permute-start = (f32[16,128]{1,0:T(8,128)S(1)}, f32[16,128]{1,0:T(8,128)S(1)}, u32[]{:S(2)}, u32[]{:S(2)}) collective-permute-start(f32[16,128]{1,0:T(8,128)S(1)} %get-tuple-element.18), channel_id=1, source_target_pairs={{0,3},{1,0},{2,1},{3,2},{4,7},{5,4},{6,5},{7,6},{8,11},{9,8},{10,9... | collective-permute-start | bytes 24584 | tf_op jit(solution)/shard_map/ppermute | solution.py:405
  7.2 0.0 collective-permute-start.1
  7.2 1.6 %collective-permute-start.2 = (f32[88,640]{1,0:T(8,128)S(1)}, f32[88,640]{1,0:T(8,128)S(1)}, u32[]{:S(2)}, u32[]{:S(2)}) collective-permute-start(f32[88,640]{1,0:T(8,128)S(1)} %get-tuple-element.23), channel_id=1, source_target_pairs={{0,28},{4,0},{8,4},{12,8},{16,12},{20,16},{24,20},{28,24},{1,29},{... | collective-permute-start | bytes 675848 | tf_op jit(solution)/shard_map/ppermute | solution.py:407
  8.8 0.0 collective-permute-start.3
  8.8 0.1 add_convert_fusion
  8.9 0.1 broadcast_in_dim.10
  8.9 0.1 broadcast_in_dim.11
  9.0 0.0 collective-permute-done.from_e
  9.0 3.6 %collective-permute-done.1.from_w = f32[16,128]{1,0:T(8,128)S(1)} collective-permute-done((f32[16,128]{1,0:T(8,128)S(1)}, f32[16,128]{1,0:T(8,128)S(1)}, u32[]{:S(2)}, u32[]{:S(2)}) %collective-permute-start.1) | collective-permute-done | bytes 8224 | tf_op jit(solution)/shard_map/ppermute | solution.py:404
  12.6 0.0 collective-permute-start.5
  12.6 2.6 %collective-permute-start.4 = (f32[32,128]{1,0:T(8,128)S(1)}, f32[32,128]{1,0:T(8,128)S(1)}, u32[]{:S(2)}, u32[]{:S(2)}) collective-permute-start(f32[32,128]{1,0:T(8,128)S(1)} %constant_dynamic-update-slice_fusion), channel_id=1, source_target_pairs={{0,28},{4,0},{8,4},{12,8},{16,12},{20,16},{24,20},{28,24},{1,29},{... | collective-permute-start | bytes 49160 | tf_op jit(solution)/shard_map/ppermute | solution.py:410
  15.3 2.8 %shard_map.87 = (f32[24,80,768]{2,1,0:T(8,128)S(1)}, f32[6,384,128]{2,1,0:T(8,128)S(1)}, f32[176,88]{1,0:T(8,128)S(1)}) custom-call(f32[16,16,640]{2,1,0:T(8,128)S(1)} %get-tuple-element.15.basis, f32[5,16,640]{2,1,0:T(8,128)S(1)} %get-tuple-element.16.sides, s32[16,640]{1,0:T(8,128)S(1)} %get-tuple-element.17.mask, ...), custom_call_target="tpu_custom_call" | custom-call | flops 1000000000 | bytes 1000000 | tf_op jit(solution)/shard_map/pallas_call | solution.py:370
  18.1 0.0 collective-permute-done.5.corner_s
  18.1 0.0 collective-permute-done.4.corner_n
  18.1 0.0 collective-permute-done.2.from_n
  18.1 0.0 collective-permute-done.3.from_s
  18.2 0.1 broadcast_in_dim.12.inside
  18.2 2.2 %shard_map.88 = (f32[32,16,128]{2,1,0:T(8,128)S(1)}, f32[6,384,128]{2,1,0:T(8,128)S(1)}, f32[24,80,768]{2,1,0:T(8,128)S(1)}, f32[6,24,768]{2,1,0:T(8,128)S(1)}) custom-call(f32[8,128]{1,0:T(8,128)S(1)} %broadcast_in_dim.12.inside, f32[6,384,128]{2,1,0:T(8,128)S(1)} %get-tuple-element.20.basis_in, ...), custom_call_target="tpu_custom_call", output_to_operand_aliasing={{1}: (1, {}), {2}: (2, {})} | custom-call | flops 1000000 | bytes 1000000 | tf_op jit(solution)/shard_map/pallas_call | solution.py:370
  20.5 12.7 %all_to_all.5.parts = f32[32,16,128]{2,1,0:T(8,128)S(1)} all-to-all(f32[32,16,128]{2,1,0:T(8,128)S(1)} %get-tuple-element.25), channel_id=1, replica_groups=mesh['lat'=8,'lon'=4] {'lat','lon'}, dimensions={0} | all-to-all | bytes 524288 | tf_op jit(solution)/shard_map/all_to_all | solution.py:436
  33.2 2.2 %shard_map.89 = (f32[16,640]{1,0:T(8,128)}, f32[16,640]{1,0:T(8,128)}) custom-call(f32[32,16,128]{2,1,0:T(8,128)S(1)} %all_to_all.5.parts, f32[5,16,640]{2,1,0:T(8,128)S(1)} %get-tuple-element.16.sides, f32[6,384,128]{2,1,0:T(8,128)S(1)} %get-tuple-element.26.basis_ext, f32[6,24,768]{2,1,0:T(8,128)S(1)} %get-tuple-element.27.side_ext), custom_call_target="tpu_custom_call" | custom-call | flops 1000000 | bytes 1000000 | tf_op jit(solution)/shard_map/pallas_call | solution.py:370
  (2 shorter events, 0.0 us)
Async XLA Ops:
  2.0 7.0 %collective-permute-start = (f32[16,128]{1,0:T(8,128)S(1)}, f32[16,128]{1,0:T(8,128)S(1)}, u32[]{:S(2)}, u32[]{:S(2)}) collective-permute-start(f32[16,128]{1,0:T(8,128)S(1)} %get-tuple-element.18), channel_id=1, source_target_pairs={{0,3},{1,0},{2,1},{3,2},{4,7},{5,4},{6,5},{7,6},{8,11},{9,8},{10,9... | collective-permute-start | bytes 24584 | tf_op jit(solution)/shard_map/ppermute | solution.py:405
  7.2 5.4 %collective-permute-start.1 = (f32[16,128]{1,0:T(8,128)S(1)}, f32[16,128]{1,0:T(8,128)S(1)}, u32[]{:S(2)}, u32[]{:S(2)}) collective-permute-start(f32[16,128]{1,0:T(8,128)S(1)} %get-tuple-element.19), channel_id=1, source_target_pairs={{0,1},{1,2},{2,3},{3,0},{4,5},{5,6},{6,7},{7,4},{8,9},{9,10},{10,1... | collective-permute-start | bytes 24584 | tf_op jit(solution)/shard_map/ppermute | solution.py:404
  7.2 11.0 %collective-permute-start.2 = (f32[88,640]{1,0:T(8,128)S(1)}, f32[88,640]{1,0:T(8,128)S(1)}, u32[]{:S(2)}, u32[]{:S(2)}) collective-permute-start(f32[88,640]{1,0:T(8,128)S(1)} %get-tuple-element.23), channel_id=1, source_target_pairs={{0,28},{4,0},{8,4},{12,8},{16,12},{20,16},{24,20},{28,24},{1,29},{... | collective-permute-start | bytes 675848 | tf_op jit(solution)/shard_map/ppermute | solution.py:407
  8.8 9.4 %collective-permute-start.3 = (f32[88,640]{1,0:T(8,128)S(1)}, f32[88,640]{1,0:T(8,128)S(1)}, u32[]{:S(2)}, u32[]{:S(2)}) collective-permute-start(f32[88,640]{1,0:T(8,128)S(1)} %get-tuple-element.24), channel_id=1, source_target_pairs={{0,4},{4,8},{8,12},{12,16},{16,20},{20,24},{24,28},{28,0},{1,5},{5... | collective-permute-start | bytes 675848 | tf_op jit(solution)/shard_map/ppermute | solution.py:406
  12.6 5.5 %collective-permute-start.5 = (f32[32,128]{1,0:T(8,128)S(1)}, f32[32,128]{1,0:T(8,128)S(1)}, u32[]{:S(2)}, u32[]{:S(2)}) collective-permute-start(f32[32,128]{1,0:T(8,128)S(1)} %constant_dynamic-update-slice_fusion), channel_id=1, source_target_pairs={{0,4},{4,8},{8,12},{12,16},{16,20},{20,24},{24,28},{28,0},{1,5},{5... | collective-permute-start | bytes 49160 | tf_op jit(solution)/shard_map/ppermute | solution.py:409
  12.6 5.5 %collective-permute-start.4 = (f32[32,128]{1,0:T(8,128)S(1)}, f32[32,128]{1,0:T(8,128)S(1)}, u32[]{:S(2)}, u32[]{:S(2)}) collective-permute-start(f32[32,128]{1,0:T(8,128)S(1)} %constant_dynamic-update-slice_fusion), channel_id=1, source_target_pairs={{0,28},{4,0},{8,4},{12,8},{16,12},{20,16},{24,20},{28,24},{1,29},{... | collective-permute-start | bytes 49160 | tf_op jit(solution)/shard_map/ppermute | solution.py:410
